TPU v7x, 128 devices: a whole 4x4x4 slice. The times are simulated.
128 devices in a mesh: tok: 64 (over z, y, x_hi, core), lay: 2 (over x_lo).
Axes of the slice: x: 4 (x_hi: 2, x_lo: 2; x = x_hi * 2 + x_lo), y: 4, z: 4, core: 2. Of those that a mesh axis runs over, the one named last changes fastest.
Arguments:
- first_acts: bfloat16 [2, 16384, 5120], P('lay', 'tok'), may hold values from -40 to 40
- second_acts: bfloat16 [2, 16384, 5120], P('lay', 'tok'), may hold values from -40 to 40
Outputs:
- whitening: float32 [2, 2, 40, 128, 128], P(None, 'lay')
- similarity: float32 [2, 2, 40], P('lay')
All inputs are finite; a program needn't handle non-finite values.
Results may differ from a plain program's by a relative error of at most 0.0003.
Values may be sent and summed in bfloat16 or wider, within the bound.
A program may use at most 128 MiB of HBM per device.

v0:
```python
import jax
import jax.numpy as jnp
from jax import lax
from jax.sharding import PartitionSpec as P

HEADS = 40
HEAD_DIM = 128
ITERS = 6


ridge_weight = 0.05
top_precision = lax.Precision.HIGHEST


def in_one(arrays, axis):
    line, at, outs = (jnp.concatenate([a.reshape(-1) for a in arrays]), 0, [])
    total = lax.psum(line, axis)
    for a in arrays:
        outs.append(total[at : at + a.size].reshape(a.shape))
        at += a.size
    return tuple(outs)


def newton_whiten(matrices):
    unit_matrix = jnp.eye(HEAD_DIM, dtype=jnp.float32)
    scale_norm = jnp.sqrt(jnp.sum(matrices * matrices, axis=(-2, -1), keepdims=True))
    square_iter = matrices / scale_norm
    inverse_iter = jnp.broadcast_to(unit_matrix, matrices.shape)
    for sweep_index in range(ITERS):
        factor_iter = 1.5 * unit_matrix - 0.5 * jnp.matmul(
            inverse_iter, square_iter, precision=top_precision
        )
        square_iter = jnp.matmul(square_iter, factor_iter, precision=top_precision)
        inverse_iter = jnp.matmul(factor_iter, inverse_iter, precision=top_precision)
    return inverse_iter / jnp.sqrt(scale_norm)


def covariance(gram_total, col_sums, token_total):
    unit_matrix = jnp.eye(HEAD_DIM, dtype=jnp.float32)
    column_mean = col_sums / token_total
    return (
        gram_total / token_total
        - column_mean[..., :, None] * column_mean[..., None, :]
        + ridge_weight * unit_matrix
    )


def partial_stats(act_block, token_rows):
    shaped = act_block.reshape(act_block.shape[0], token_rows, HEADS, HEAD_DIM)
    gram_part = jnp.einsum("lthi,lthj->lhij", shaped, shaped, preferred_element_type=jnp.float32)
    col_sums = jnp.sum(shaped, axis=1, dtype=jnp.float32)
    return (gram_part, col_sums)


def local(first_acts, second_acts):
    lay_dev = first_acts.shape[0]
    token_rows = first_acts.shape[1]
    token_total = token_rows * lax.axis_size("tok")
    gathered = lax.all_gather(second_acts, "lay", axis=0, tiled=True)
    gram_first, sums_first = partial_stats(first_acts, token_rows)
    gram_second, sums_second = partial_stats(second_acts, token_rows)
    gram_total, sums_total = in_one(
        (jnp.stack([gram_first, gram_second]), jnp.stack([sums_first, sums_second])), "tok"
    )
    whitening = newton_whiten(covariance(gram_total, sums_total, token_total))
    white_first = whitening[0]
    sums_first = sums_total[0]
    white_second, sums_second = (
        lax.all_gather(whitening[1], "lay", axis=0, tiled=True),
        lax.all_gather(sums_total[1], "lay", axis=0, tiled=True),
    )
    mean_first = sums_first / token_total
    mean_second = sums_second / token_total
    view_first = first_acts.reshape(lay_dev, token_rows, HEADS, HEAD_DIM)
    view_second = gathered.reshape(gathered.shape[0], token_rows, HEADS, HEAD_DIM)
    cross_part = jnp.einsum(
        "athi,bthj->abhij", view_first, view_second, preferred_element_type=jnp.float32
    )
    cross_sum = lax.psum(cross_part, "tok")
    cross_cov = (
        cross_sum / token_total - mean_first[:, None, :, :, None] * mean_second[None, :, :, None, :]
    )
    left_product = jnp.matmul(white_first[:, None], cross_cov, precision=top_precision)
    whitened = jnp.matmul(left_product, white_second[None], precision=top_precision)
    similarity = jnp.sum(whitened * whitened, axis=(-2, -1)) / HEAD_DIM
    return (whitening, similarity)


def solution(mesh):
    in_specs = (P("lay", "tok", None), P("lay", "tok", None))
    out_specs = (P(None, "lay", None, None, None), P("lay", None, None))
    return jax.shard_map(local, mesh=mesh, in_specs=in_specs, out_specs=out_specs, check_vma=False)
```

profile of v0, /device:TPU:1, one launch (start us, length us, event | category | flops | bytes accessed | tf_op | source)
XLA Modules:
  0.0 982.1 jit_solution(11143074356550692935)
XLA Ops:
  7.2 0.0 copy-start.3
  7.2 0.0 all-gather.3.cloned.1.call-start
  7.2 0.7 all-gather.3.cloned.1.call-update
  7.9 0.0 all-reduce.3.cloned.1.call-start
  8.0 2.2 convert_reduce_fusion
  10.1 0.0 copy-done.3
  10.1 0.4 convert_reduce_fusion.1
  10.6 0.0 copy-start
  10.6 0.5 copy.43
  11.1 0.0 copy-start.1
  11.1 1.1 fusion.58
  12.2 0.7 copy-done
  12.9 0.5 copy.44
  13.4 0.0 copy-done.1
  13.4 1.1 fusion.61
  14.5 0.6 pad_maximum_fusion.1
  15.2 3.3 pad_maximum_fusion
  18.5 0.0 copy-start.2
  18.5 65.3 %all-gather.3.cloned.1.call-done = bf16[2,256,5120]{2,1,0:T(8,128)(2,1)} async-done(((bf16[1,256,5120]{2,1,0:T(8,128)(2,1)}), bf16[2,256,5120]{2,1,0:T(8,128)(2,1)}) %all-gather.3.cloned.1.call-update) | async-done | bytes 5242896 | tf_op jit(solution)/shard_map/all_gather | solution.py:59
  83.7 7.9 copy.32
  91.7 0.0 copy-done.2
  91.7 6.3 fusion.51
  97.9 0.0 all-reduce.3.cloned.1.call-update
  98.0 0.0 all-gather.5.cloned.1.call-start
  98.1 668.4 %all-reduce.3.cloned.1.call-done = (f32[1320960]{0:T(1024)}, f32[1,2,40,128,128]{3,4,1,2,0:T(8,128)}) async-done(((f32[1320960]{0:T(1024)}, f32[1,2,40,128,128]{3,4,1,2,0:T(8,128)}), (f32[1320960]{0:T(1024)}, f32[1,2,40,128,128]{3,4,1,2,0:T(8,128)})) %all-reduce.3.cloned.1.call-update) | async-done | bytes 10526736 | tf_op jit(solution)/shard_map/psum | solution.py:17
  766.4 0.8 slice_multiply_fusion.1
  767.2 2.7 slice_multiply_fusion
  769.9 3.1 multiply_reduce_fusion.1
  773.0 5.9 fusion.38
  778.9 7.9 fusion.9
  786.8 5.6 fusion.10
  792.4 6.7 fusion.80
  799.1 7.1 fusion.11
  806.1 7.5 fusion.12
  813.7 6.7 fusion.81
  820.3 7.0 fusion.13
  827.4 7.1 fusion.14
  834.5 6.9 fusion.82
  841.4 6.9 fusion.15
  848.3 7.5 fusion.16
  855.8 6.7 fusion.83
  862.5 7.3 fusion.18
  869.7 6.9 fusion.17
  876.6 6.9 fusion.84
  883.5 7.0 broadcast_divide_fusion
  890.5 0.0 copy-start.4
  890.5 2.3 copy-done.4
  892.9 1.8 slice.66
  894.6 0.0 all-gather.5.cloned.1.call-update
  894.7 0.8 fusion.67
  895.4 3.7 all_gather.10
  899.1 9.5 fusion.2
  908.6 57.5 %all-gather.5.cloned.1.call-done = f32[2,40,128,128]{3,2,1,0:T(8,128)} async-done(((f32[1,40,128,128]{3,2,1,0:T(8,128)}), f32[2,40,128,128]{3,2,1,0:T(8,128)}) %all-gather.5.cloned.1.call-update) | async-done | bytes 5242896 | tf_op jit(solution)/shard_map/all_gather | solution.py:69
  966.1 8.4 multiply_reduce_fusion
  974.5 0.6 multiply_bitcast_fusion
  (7 shorter events, 0.1 us)
Async XLA Ops:
  7.2 3.0 copy-start.3
  7.2 76.6 %all-gather.3.cloned.1.call-start = ((), (), s32[]{:S(2)}) async-start(), calls=%async_computation | async-start | bytes 7864320 | tf_op jit(solution)/shard_map/all_gather | solution.py:59
  7.9 758.5 %all-reduce.3.cloned.1.call-start = ((), (), s32[]{:S(2)}) async-start(), calls=%async_computation.2 | async-start | bytes 21053440 | tf_op jit(solution)/shard_map/psum | solution.py:17
  10.6 2.3 copy-start
  11.1 2.3 copy-start.1
  18.5 73.2 %copy-start.2 = (bf16[32,8,40,128]{3,2,1,0:T(8,128)(2,1)S(1)}, bf16[32,8,40,128]{3,2,1,0:T(8,128)(2,1)}, u32[]{:S(2)}) copy-start(bf16[32,8,40,128]{3,2,1,0:T(8,128)(2,1)} %copy-done.1) | copy-start | bytes 7864324
  98.0 868.2 %all-gather.5.cloned.1.call-start = ((), (), s32[]{:S(2)}) async-start(), calls=%async_computation.1 | async-start | bytes 7864320 | tf_op jit(solution)/shard_map/all_gather | solution.py:69
  890.5 2.4 copy-start.4
Sparse Core Ops, SparseCore 0:
  9.6 74.0 all-gather.2
  98.1 668.2 all-reduce.2
  894.8 71.2 all-gather.4
where the time goes:
time: 988 us; the launch traced here: 982 us
  waiting for transfers between devices  792 us (80%)
  matrix products  144 us (15%)
  other arithmetic  14.5 us (1%)
  between operations  14.5 us (1%)
  local copies, waits for them, and re-layouts  13.8 us (1%)
    psum x1, waiting for transfers between devices, in_one(): total = lax.psum(line, axis)  668 us
    all_gather x1, waiting for transfers between devices, local(): gathered = lax.all_gather(second_acts, 'lay', axis=0, tiled=True)  65.3 us
    all_gather x1, waiting for transfers between devices, local(): lax.all_gather(whitening[1], 'lay', axis=0, tiled=True)  57.5 us
    dot_general x6, matrix products, newton_whiten(): jnp.matmul(factor_iter, inverse_iter, precision=top_precision)  42 us
    dot_general x6, matrix products, newton_whiten(): jnp.matmul(inverse_iter, square_iter, precision=top_precision)  39.6 us
    dot_general x5, matrix products, newton_whiten(): square_iter = jnp.matmul(square_iter, factor_iter, precision=top_precision)  35.7 us
  transfers between devices with their start and end apart: 3, of which 3 were waited for; matrix products, arithmetic and copies ran while one was open for 2% of the time, Pallas kernels for 0%

commit v1 on v0

v1 whole, which is shorter than its diff:
```python
import functools

import jax
import jax.numpy as jnp
from jax import lax
from jax.experimental import pallas as pl
from jax.experimental.pallas import tpu as pltpu
from jax.sharding import PartitionSpec as P

HEADS = 40
HD = 128
ITERS = 6
RIDGE = 0.05
HALF = HEADS // 2
PARTS = 4
PART_HEADS = HEADS // PARTS
F32 = jnp.float32
HI = lax.Precision.HIGHEST
MESH = pl.DeviceIdType.MESH

CHAINS = {
    "pa": (72, "z"),
    "pb": (64, "y"),
    "ca": (64, "z"),
    "cb": (64, "y"),
    "da": (64, "z"),
    "db": (64, "y"),
}
GATHERS = {"wa": (72, "z"), "wb": (64, "y"), "sa": (8, "z")}


def iota(shape, dim):
    return lax.broadcasted_iota(jnp.int32, shape, dim)


def dot_t(a, b, precision=None):
    return lax.dot_general(
        a, b, (((0,), (0,)), ((), ())), precision=precision, preferred_element_type=F32
    )


def mm(a, b):
    return jnp.dot(a, b, precision=HI, preferred_element_type=F32)


def kernel(tokens, names, *refs):
    r = dict(zip(names, refs))
    tok = lax.axis_index("tok")
    lay = lax.axis_index("lay")
    c = tok % 2
    xh = (tok // 2) % 2
    y = (tok // 4) % 4
    z = tok // 16

    def dev(z_, y_, xh_, c_):
        return (((z_ * 4 + y_) * 2 + xh_) * 2 + c_, lay)

    def dev_uv(axis, u, v, xh_):
        return dev(u, v, xh_, c) if axis == "z" else dev(v, u, xh_, c)

    def uv(axis):
        return (z, y) if axis == "z" else (y, z)

    sibling = dev(z, y, xh, 1 - c)
    twin = (tok, 1 - lay)

    owner = jnp.logical_or(xh == (z + y) % 2, jnp.logical_and(z == y, xh == 1))

    def own_slot(axis):
        u, v = uv(axis)
        return jnp.where(xh == (z + y) % 2, v, 4)

    def slot_owner(axis, s):
        u, _ = uv(axis)
        vo = s if s < 4 else u
        xo = (u + vo) % 2 if s < 4 else 1
        return u, vo, xo

    def rcopy(src, dst, ssem, rsem, device):
        return pltpu.make_async_remote_copy(
            src_ref=src, dst_ref=dst, send_sem=ssem, recv_sem=rsem,
            device_id=device, device_id_type=MESH,
        )

    pending = []

    def launch(copy):
        copy.start()
        pending.append(copy)
        return copy

    def s1(name):
        q = lambda k: r[name + k]
        return rcopy(q("").at[1 - c], q("_r1"), q("_s").at[0], q("_q").at[0], sibling)

    def s1_sum(name):
        buf, r1 = r[name], r[name + "_r1"]
        s1(name).wait_recv()

        def body(i, carry):
            for s in range(5):
                buf[c, i, s] = buf[c, i, s] + r1[i, s]
            return carry

        lax.fori_loop(0, 4, body, 0)

    def s2(name, d):
        axis = CHAINS[name][1]
        u, v = uv(axis)
        to = (u + d) % 4
        q = lambda k: r[name + k]
        return rcopy(
            q("").at[c, to], q("_r2").at[d - 1], q("_s").at[d], q("_q").at[d],
            dev_uv(axis, to, v, xh),
        )

    def s2_sum(name):
        axis = CHAINS[name][1]
        u, _ = uv(axis)
        buf, r2, acc = r[name], r[name + "_r2"], r[name + "_acc"]
        for d in (1, 2, 3):
            s2(name, d).wait_recv()
        for s in range(5):
            acc[s] = (buf[c, u, s] + r2[0, s]) + (r2[1, s] + r2[2, s])

    def s3(name, s):
        axis = CHAINS[name][1]
        u, v = uv(axis)
        _, vo, xo = slot_owner(axis, s)
        slot = ((v - vo + 4) % 4) * 2 + (xh + xo) % 2
        mine = jnp.logical_and(v == vo, xh == xo)
        q = lambda k: r[name + k]
        copy = rcopy(
            q("_acc").at[s], q("_r3").at[slot], q("_s").at[4 + s], q("_q").at[4 + slot],
            dev_uv(axis, u, vo, xo),
        )
        return mine, copy

    def s3_start(name):
        for s in range(5):
            mine, copy = s3(name, s)

            @pl.when(jnp.logical_not(mine))
            def _():
                copy.start()

    def s3_total(name):
        axis = CHAINS[name][1]
        r3 = r[name + "_r3"]
        total = r[name + "_acc"][own_slot(axis)]
        for slot in range(1, 8):
            rcopy(r3.at[slot], r3.at[slot], r[name + "_s"].at[0], r[name + "_q"].at[4 + slot], twin).wait_recv()
        for slot in range(1, 8):
            total = total + r3[slot]
        return total

    def s3_drain(name):
        for s in range(5):
            mine, copy = s3(name, s)

            @pl.when(jnp.logical_not(mine))
            def _():
                copy.wait_send()

    def g1(name, i):
        axis = GATHERS[name][1]
        u, v = uv(axis)
        mine = own_slot(axis)
        place = r[name].at[c, u, mine]
        return rcopy(
            place, place, r[name + "_s"].at[i], r[name + "_q"].at[mine],
            dev_uv(axis, u, (v + i // 2) % 4, (xh + i % 2) % 2),
        )

    def g1_start(name):
        for i in range(1, 8):
            g1(name, i).start()

    def g1_wait(name):
        axis = GATHERS[name][1]
        u, _ = uv(axis)
        for s in range(5):
            place = r[name].at[c, u, s]

            @pl.when(jnp.logical_not(jnp.logical_and(owner, own_slot(axis) == s)))
            def _():
                rcopy(place, place, r[name + "_s"].at[0], r[name + "_q"].at[s], twin).wait_recv()

    def g2(name, d):
        axis = GATHERS[name][1]
        u, v = uv(axis)
        place = r[name].at[c, u]
        return rcopy(
            place, place, r[name + "_s"].at[7 + d], r[name + "_q"].at[4 + d],
            dev_uv(axis, (u + d) % 4, v, xh),
        )

    def g3(name):
        place = r[name].at[c]
        return rcopy(place, place, r[name + "_s"].at[11], r[name + "_q"].at[8], sibling)

    def exchange(e):
        cols = pl.ds(e * PART_HEADS * HD, PART_HEADS * HD)
        return rcopy(
            r["x2_hbm"].at[0, :, cols], r["x2o"].at[:, cols],
            r["x_s"].at[e], r["x_q"].at[e], twin,
        )

    barrier = pltpu.get_barrier_semaphore()
    peers = [sibling, twin]
    for i in range(1, 8):
        peers.append(dev(z, (y + i // 2) % 4, (xh + i % 2) % 2, c))
    for i in range(2, 8):
        peers.append(dev((z + i // 2) % 4, y, (xh + i % 2) % 2, c))
    for peer in peers:
        pl.semaphore_signal(barrier, inc=1, device_id=peer, device_id_type=MESH)
    load1 = pltpu.make_async_copy(r["x1_hbm"].at[0], r["x1"], r["l_s"].at[0])
    load2 = pltpu.make_async_copy(r["x2_hbm"].at[0], r["x2"], r["l_s"].at[1])
    load1.start()
    load2.start()
    pl.semaphore_wait(barrier, len(peers))

    launch(exchange(0))
    launch(exchange(1))
    load1.wait()
    load2.wait()

    ri = iota((HD, HD), 0)
    ci = iota((HD, HD), 1)
    row8 = iota((8, HD), 0)
    upper = ri <= ci
    diag = ri == ci
    eye = jnp.where(diag, 1.0, 0.0).astype(F32)
    x1, x2, x2o = r["x1"], r["x2"], r["x2o"]

    def places(h):
        k = h % HALF
        main = k < 16
        return (
            h // HALF,
            k % 4,
            k // 4,
            jnp.where(main, k // 4, k % 4),
            jnp.where(main, k % 4, 4),
        )

    def gram(h):
        ch, zz, ss, yy, rr = places(h)
        cols = pl.ds(pl.multiple_of(h * HD, HD), HD)
        ab = jnp.concatenate([x1[:, cols], x2[:, cols]], axis=1)
        g = dot_t(ab, ab)
        sums = jnp.dot(jnp.ones((8, ab.shape[0]), ab.dtype), ab, preferred_element_type=F32)
        g1_, cr, g2_ = g[:HD, :HD], g[:HD, HD:], g[HD:, HD:]
        p = jnp.where(upper, g1_, g2_)
        dg = jnp.sum(jnp.where(diag, g2_, 0.0), axis=0, keepdims=True)
        aux = jnp.where(
            row8 == 0, sums[:, :HD],
            jnp.where(row8 == 1, sums[:, HD:], jnp.where(row8 == 2, jnp.broadcast_to(dg, (8, HD)), 0.0)),
        )
        r["pa"][ch, zz, ss, 0:64] = p[:64]
        r["pa"][ch, zz, ss, 64:72] = aux
        r["pb"][ch, yy, rr] = p[64:]
        r["ca"][ch, zz, ss] = cr[:64]
        r["cb"][ch, yy, rr] = cr[64:]

    def loop(lo, n, body):
        def step(i, carry):
            body(lo + i)
            return carry

        lax.fori_loop(0, n, step, 0)

    loop((1 - c) * HALF, HALF, gram)
    for name in ("pa", "pb", "ca", "cb"):
        launch(s1(name))
    loop(c * HALF, HALF, gram)
    for name in ("pa", "pb", "ca", "cb"):
        s1_sum(name)
        for d in (1, 3, 2):
            launch(s2(name, d))
    for name in ("pa", "pb"):
        s2_sum(name)
        s3_start(name)
    launch(exchange(2))

    def unpack(top, low, aux):
        p = jnp.concatenate([top, low], axis=0)
        pt = p.T
        first = jnp.where(upper, p, pt)
        second = jnp.where(upper, jnp.where(diag, aux[2:3, :], pt), p)
        return first, second

    def only_row0(row):
        return jnp.where(row8 == 0, jnp.broadcast_to(row, (8, HD)), 0.0)

    @pl.when(owner)
    def _():
        top = s3_total("pa")
        low = s3_total("pb")
        aux = top[64:72]
        grams = unpack(top[:64], low, aux)
        ys, zs, scales = [], [], []
        for n in (0, 1):
            mean = only_row0(aux[n : n + 1, :]) / tokens
            cov = grams[n] / tokens - dot_t(mean, mean, HI) + RIDGE * eye
            sq = jnp.sum(jnp.sum(cov * cov, axis=1, keepdims=True), axis=0, keepdims=True)
            scale = jnp.sqrt(sq)
            scales.append(scale)
            ys.append(cov / scale)
        for it in range(ITERS):
            for n in (0, 1):
                if it == 0:
                    f = 1.5 * eye - 0.5 * ys[n]
                    zs.append(f)
                else:
                    f = 1.5 * eye - 0.5 * mm(zs[n], ys[n])
                    zs[n] = mm(f, zs[n])
                if it < ITERS - 1:
                    ys[n] = mm(ys[n], f)
        w1 = zs[0] / jnp.sqrt(scales[0])
        w2 = zs[1] / jnp.sqrt(scales[1])
        wp = jnp.where(upper, w1, w2)
        wd = jnp.sum(jnp.where(diag, w2, 0.0), axis=0, keepdims=True)
        slot_z, slot_y = own_slot("z"), own_slot("y")
        r["wa"][c, z, slot_z, 0:64] = wp[:64]
        r["wa"][c, z, slot_z, 64:72] = jnp.broadcast_to(wd, (8, HD))
        r["wb"][c, y, slot_y] = wp[64:]
        r["w12"][0] = w1
        r["w12"][1] = w2
        r["aux"][...] = aux
        r["w_out_x"][0:HD] = w2
        r["w_out_x"][HD : HD + 8] = aux
        g1_start("wa")
        g1_start("wb")
        rcopy(r["w_out_x"], r["w_in_x"], r["y_s"].at[0], r["y_q"].at[0], twin).start()

    launch(exchange(3))
    for name in ("ca", "cb"):
        s2_sum(name)
        s3_start(name)
    for name in ("wa", "wb"):
        g1_wait(name)
        for d in (1, 3, 2):
            launch(g2(name, d))

    def cross(h):
        ch, zz, ss, yy, rr = places(h)
        cols = pl.ds(pl.multiple_of(h * HD, HD), HD)
        cr = dot_t(x1[:, cols], x2o[:, cols])
        r["da"][ch, zz, ss] = cr[:64]
        r["db"][ch, yy, rr] = cr[64:]

    for e in range(2):
        exchange(e).wait_recv()
        loop(e * PART_HEADS, PART_HEADS, cross)
    for name in ("wa", "wb"):
        for d in (1, 3, 2):
            g2(name, d).wait_recv()
        launch(g3(name))
    for e in range(2, PARTS):
        exchange(e).wait_recv()
        loop(e * PART_HEADS, PART_HEADS, cross)
    for name in ("da", "db"):
        launch(s1(name))
    for name in ("da", "db"):
        s1_sum(name)
        for d in (1, 3, 2):
            launch(s2(name, d))

    for name in ("wa", "wb"):
        g3(name).wait_recv()

    def emit(h):
        ch, zz, ss, yy, rr = places(h)
        w1, w2 = unpack(r["wa"][ch, zz, ss, 0:64], r["wb"][ch, yy, rr], r["wa"][ch, zz, ss, 64:72])
        r["w_ref"][0, 0, h] = w1
        r["w_ref"][1, 0, h] = w2

    loop(0, HEADS, emit)

    for name in ("da", "db"):
        s2_sum(name)
        s3_start(name)

    @pl.when(owner)
    def _():
        own = jnp.concatenate([s3_total("ca"), s3_total("cb")], axis=0)
        rcopy(r["w_out_x"], r["w_in_x"], r["y_s"].at[0], r["y_q"].at[0], twin).wait()
        other = jnp.concatenate([s3_total("da"), s3_total("db")], axis=0)
        aux = r["aux"][...]
        mean1 = only_row0(aux[0:1, :]) / tokens
        sims = []
        for raw, sums, w2 in (
            (own, aux[1:2, :], r["w12"][1]),
            (other, r["w_in_x"][HD + 1 : HD + 2], r["w_in_x"][0:HD]),
        ):
            cov = raw / tokens - dot_t(mean1, only_row0(sums) / tokens, HI)
            white = mm(mm(r["w12"][0], cov), w2)
            sq = jnp.sum(jnp.sum(white * white, axis=1, keepdims=True), axis=0, keepdims=True)
            sims.append(sq / HD)
        k = jnp.where(own_slot("z") < 4, 4 * own_slot("z") + z, 16 + z)
        here = iota((8, HD), 1) == c * HALF + k
        tile = jnp.where(row8 == lay, jnp.broadcast_to(sims[0], (8, HD)), 0.0)
        tile = jnp.where(row8 == 1 - lay, jnp.broadcast_to(sims[1], (8, HD)), tile)
        r["sa"][c, z, own_slot("z")] = jnp.where(here, tile, 0.0)
        g1_start("sa")

    g1_wait("sa")
    for d in (1, 3, 2):
        launch(g2("sa", d))
    for d in (1, 2, 3):
        g2("sa", d).wait_recv()
    launch(g3("sa"))
    g3("sa").wait_recv()
    total = jnp.zeros((8, HD), F32)
    for ch in range(2):
        for i in range(4):
            for s in range(5):
                total = total + r["sa"][ch, i, s]
    r["s_ref"][0] = total[0:2, 0:HEADS]

    for copy in pending:
        copy.wait_send()
    for name in CHAINS:
        s3_drain(name)

    @pl.when(owner)
    def _():
        for name in GATHERS:
            for i in range(1, 8):
                g1(name, i).wait_send()


def local(tokens, first_acts, second_acts):
    rows, width = first_acts.shape[1:]
    names = ["x1_hbm", "x2_hbm", "w_ref", "s_ref"]
    scratch = []

    def add(name, spec):
        names.append(name)
        scratch.append(spec)

    dma = lambda n: pltpu.SemaphoreType.DMA((n,))
    for name in ("x1", "x2", "x2o"):
        add(name, pltpu.VMEM((rows, width), first_acts.dtype))
    for name, (n, _) in CHAINS.items():
        add(name, pltpu.VMEM((2, 4, 5, n, HD), F32))
        add(name + "_r1", pltpu.VMEM((4, 5, n, HD), F32))
        add(name + "_r2", pltpu.VMEM((3, 5, n, HD), F32))
        add(name + "_acc", pltpu.VMEM((5, n, HD), F32))
        add(name + "_r3", pltpu.VMEM((8, n, HD), F32))
        add(name + "_s", dma(9))
        add(name + "_q", dma(12))
    for name, (n, _) in GATHERS.items():
        add(name, pltpu.VMEM((2, 4, 5, n, HD), F32))
        add(name + "_s", dma(12))
        add(name + "_q", dma(9))
    add("w12", pltpu.VMEM((2, HD, HD), F32))
    add("aux", pltpu.VMEM((8, HD), F32))
    add("w_out_x", pltpu.VMEM((HD + 8, HD), F32))
    add("w_in_x", pltpu.VMEM((HD + 8, HD), F32))
    add("l_s", dma(2))
    add("x_s", dma(PARTS))
    add("x_q", dma(PARTS))
    add("y_s", dma(1))
    add("y_q", dma(1))
    return pl.pallas_call(
        functools.partial(kernel, tokens, names),
        out_shape=(
            jax.ShapeDtypeStruct((2, 1, HEADS, HD, HD), F32),
            jax.ShapeDtypeStruct((1, 2, HEADS), F32),
        ),
        in_specs=[pl.BlockSpec(memory_space=pl.ANY)] * 2,
        out_specs=(
            pl.BlockSpec(memory_space=pltpu.VMEM),
            pl.BlockSpec(memory_space=pltpu.VMEM),
        ),
        scratch_shapes=scratch,
        compiler_params=pltpu.CompilerParams(collective_id=0, has_side_effects=True),
    )(first_acts, second_acts)


def solution(mesh):
    def whole(first_acts, second_acts):
        tokens = first_acts.shape[1] * lax.axis_size("tok")
        return local(tokens, first_acts, second_acts)

    in_specs = (P("lay", "tok", None), P("lay", "tok", None))
    out_specs = (P(None, "lay", None, None, None), P("lay", None, None))
    return jax.shard_map(whole, mesh=mesh, in_specs=in_specs, out_specs=out_specs, check_vma=False)
```

time: 988 us -> 121 us (0.12)
  waiting for transfers between devices: 792 us -> 0 us
  matrix products: 144 us -> 0 us
  Pallas kernels: 0 us -> 114 us
  other arithmetic: 14.5 us -> 0 us
  between operations: 14.5 us -> 0.65 us
    psum x1 -> x0, waiting for transfers between devices: 668 us -> none  [in_one(): total = lax.psum(line, axis)]
    dot_general x22 -> x0, matrix products: 144 us -> none  [the longest x6 42 us: newton_whiten(): jnp.matmul(factor_iter, inverse_iter, precision=top_precision)]
    all_gather x2 -> x0, waiting for transfers between devices: 123 us -> none  [the longest x1 65.3 us: local(): gathered = lax.all_gather(second_acts, 'lay', axis=0, tiled=True)]
    pallas_call x0 -> x1, Pallas kernels: none -> 114 us  [local(): pl.pallas_call(functools.partial(kernel, tokens, names), out_shape=(jax.S...]
  transfers between devices with their start and end apart: 3 -> 0, of which waited for: 3 -> 0; matrix products, arithmetic and copies ran while one was open for 2% -> 0% of each run, Pallas kernels for 0% -> 0%
where the time goes in v1:
time: 121 us; the launch traced here: 120 us
  Pallas kernels  114 us (94%)
  local copies, waits for them, and re-layouts  6.05 us (5%)
    pallas_call x1, Pallas kernels, local(): pl.pallas_call(functools.partial(kernel, tokens, names), out_shape=(jax.S...  114 us
    unnamed x4, local copies, waits for them, and re-layouts  6.05 us

profile of v1, /device:TPU:1, one launch (start us, length us, event | category | flops | bytes accessed | tf_op | source)
XLA Modules:
  0.0 120.5 jit_solution(1225340315449018239)
XLA Ops:
  0.6 113.8 %shard_map.41 = (f32[2,1,40,128,128]{4,3,2,1,0:T(8,128)}, f32[1,2,40]{2,1,0:T(2,128)}) custom-call(bf16[1,256,5120]{2,1,0:T(8,128)(2,1)} %refs_0_.1, bf16[1,256,5120]{2,1,0:T(8,128)(2,1)} %refs_1_.1), custom_call_target="tpu_custom_call" | custom-call | tf_op jit(solution)/shard_map/pallas_call | solution.py:467
  114.4 0.0 copy-start
  114.4 5.5 %copy.6 = f32[2,1,40,128,128]{4,3,2,1,0:T(8,128)} copy(f32[2,1,40,128,128]{4,3,2,1,0:T(8,128)} %get-tuple-element.4) | data formatting | bytes 10485760
  119.9 0.0 copy-done
  119.9 0.6 copy.7
Async XLA Ops:
  114.4 5.5 %copy-start = (f32[1,2,40]{2,1,0:T(2,128)S(1)}, f32[1,2,40]{2,1,0:T(2,128)}, u32[]{:S(2)}) copy-start(f32[1,2,40]{2,1,0:T(2,128)} %get-tuple-element.5) | copy-start | bytes 964

commit v2 on v0

v2 whole, which is shorter than its diff:
```python
import functools

import jax
import jax.numpy as jnp
from jax import lax
from jax.experimental import pallas as pl
from jax.experimental.pallas import tpu as pltpu
from jax.sharding import PartitionSpec as P

HEADS = 40
HD = 128
ITERS = 6
RIDGE = 0.05
HALF = HEADS // 2
PARTS = 5
FROM_HBM = 3
BATCHES = (14, 19, 27)
VMEM_LIMIT = 48 * 2**20
F32 = jnp.float32
HI = lax.Precision.HIGHEST
MESH = pl.DeviceIdType.MESH

CHAINS = {"pa": (72, "z"), "pb": (64, "y"), "ca": (64, "z"), "cb": (64, "y")}
LATE = {"da": "z", "db": "y"}
GATHERS = {"wa": (72, "z"), "wb": (64, "y")}


def iota(shape, dim):
    return lax.broadcasted_iota(jnp.int32, shape, dim)


def dot_t(a, b, precision=None):
    return lax.dot_general(
        a, b, (((0,), (0,)), ((), ())), precision=precision, preferred_element_type=F32
    )


def mm(a, b):
    return jnp.dot(a, b, precision=HI, preferred_element_type=F32)


def masks():
    ri, ci = iota((HD, HD), 0), iota((HD, HD), 1)
    return ri <= ci, ri == ci


def unpack(top, low, aux):
    upper, diag = masks()
    p = jnp.concatenate([top, low], axis=0)
    pt = p.T
    first = jnp.where(upper, p, pt)
    second = jnp.where(upper, jnp.where(diag, aux[2:3, :], pt), p)
    return first, second


def head_of(z, p):
    k = 4 * ((z + p) % 4) + z
    if isinstance(p, int):
        return 16 + z if p == 4 else k
    return jnp.where(p == 4, 16 + z, k)


def places(h):
    k = h % HALF
    z = k % 4
    y = jnp.where(k < 16, k // 4, z)
    p = jnp.where(k < 16, (k // 4 - z + 4) % 4, 4)
    return h // HALF, z, y, p


def kernel(tokens, names, *refs):
    r = dict(zip(names, refs))
    tok = lax.axis_index("tok")
    lay = lax.axis_index("lay")
    c = tok % 2
    xh = (tok // 2) % 2
    y = (tok // 4) % 4
    z = tok // 16

    def dev(z_, y_, xh_, c_):
        return (((z_ * 4 + y_) * 2 + xh_) * 2 + c_, lay)

    def uv(axis):
        return (z, y) if axis == "z" else (y, z)

    def dev_uv(axis, u, v, xh_):
        return dev(u, v, xh_, c) if axis == "z" else dev(v, u, xh_, c)

    sibling = dev(z, y, xh, 1 - c)
    twin = (tok, 1 - lay)
    far = dev(z, y, 1 - xh, c)

    on_diag = z == y
    main = (y - z + 4) % 4
    owns_main = xh == main % 2
    owner = jnp.logical_or(owns_main, on_diag)
    own = jnp.where(owns_main, main, 4)
    late_owner = jnp.logical_and(on_diag, xh == 1)
    early_owner = owns_main
    extra_mine = jnp.where(owns_main, 0, 1)
    extra_give = jnp.where(owns_main, 1, 0)
    gives = jnp.logical_or(on_diag, jnp.logical_not(owns_main))
    no = jnp.logical_not

    def target(axis, p):
        u, _ = uv(axis)
        if p == 4:
            return u
        return (u + p) % 4 if axis == "z" else (u - p + 4) % 4

    def rcopy(src, dst, ssem, rsem, device):
        return pltpu.make_async_remote_copy(
            src_ref=src, dst_ref=dst, send_sem=ssem, recv_sem=rsem,
            device_id=device, device_id_type=MESH,
        )

    pending = []

    def launch(copy, cond=None):
        pending.append((cond, copy))
        if cond is None:
            copy.start()
        else:
            pl.when(cond)(lambda: copy.start())

    def arrive(ref, sem, cond=None):
        copy = rcopy(ref, ref, r["none"].at[0], sem, twin)
        if cond is None:
            copy.wait_recv()
        else:
            pl.when(cond)(lambda: copy.wait_recv())

    def loop(n, body, unroll=1):
        def step(i, carry):
            body(i)
            return carry

        lax.fori_loop(0, n, step, 0, unroll=unroll)

    def s1(name):
        launch(rcopy(r[name].at[1 - c], r[name + "_r1"], r[name + "_s"].at[0], r[name + "_q"].at[0], sibling))

    def s1_sum(name):
        buf, r1 = r[name], r[name + "_r1"]
        arrive(r1, r[name + "_q"].at[0])

        def body(i):
            for s in range(5):
                buf[c, i, s] = buf[c, i, s] + r1[i, s]

        loop(4, body)

    def s2(name):
        axis = CHAINS[name][1]
        u, v = uv(axis)
        for d in (1, 3, 2):
            to = (u + d) % 4
            launch(
                rcopy(
                    r[name].at[c, to], r[name + "_r2"].at[d - 1], r[name + "_s"].at[d],
                    r[name + "_q"].at[d], dev_uv(axis, to, v, xh),
                )
            )

    def s2_sum(name):
        u, _ = uv(CHAINS[name][1])
        buf, r2, acc = r[name], r[name + "_r2"], r[name + "_acc"]
        for d in (1, 2, 3):
            arrive(r2.at[d - 1], r[name + "_q"].at[d])
        for s in range(5):
            acc[s] = (buf[c, u, s] + r2[0, s]) + (r2[1, s] + r2[2, s])

    def s3(name, axis, slots):
        u, v = uv(axis)
        for p in slots:
            vo = target(axis, p)
            off = jnp.maximum((v - vo + 4) % 4, 1) - 1
            kind = p // 4
            launch(
                rcopy(
                    r[name + "_acc"].at[p], r[name + "_r3"].at[kind, off], r[name + "_s"].at[4 + p],
                    r[name + "_q"].at[4 + kind * 3 + off], dev_uv(axis, u, vo, xh),
                ),
                v != vo,
            )

    def s3_sum(name, extra):
        acc, r3, part = r[name + "_acc"], r[name + "_r3"], r[name + "_t"]

        def add(kind, slot):
            for off in range(3):
                arrive(r3.at[kind, off], r[name + "_q"].at[4 + kind * 3 + off])
            part[kind] = (acc[slot] + r3[kind, 0]) + (r3[kind, 1] + r3[kind, 2])

        add(0, main)
        if extra:
            pl.when(on_diag)(lambda: add(1, 4))

    def s4(name, extra):
        src = r[name + "_t"].at[extra_give] if extra else r[name + "_t"].at[0]
        cond = gives if extra else no(owns_main)
        launch(rcopy(src, r[name + "_r4"], r[name + "_s"].at[9], r[name + "_q"].at[10], far), cond)

    def s4_total(name, extra):
        arrive(r[name + "_r4"], r[name + "_q"].at[10])
        mine = r[name + "_t"][extra_mine] if extra else r[name + "_t"][0]
        return mine + r[name + "_r4"][...]

    def g1(name):
        u, _ = uv(GATHERS[name][1])
        place = r[name].at[c, u, own]
        rcopy(place, place, r[name + "_s"].at[0], r[name + "_q"].at[0], far).start()

    def g1_arrive(name):
        u, _ = uv(GATHERS[name][1])
        arrive(r[name].at[c, u, jnp.where(owns_main, 4, main)], r[name + "_q"].at[0], gives)

    def g2(name):
        axis = GATHERS[name][1]
        u, v = uv(axis)
        for d in (1, 3, 2):
            for kind in (0, 1):
                slot = 4 if kind else main
                place = r[name].at[c, u, slot]
                launch(
                    rcopy(
                        place, place, r[name + "_s"].at[kind * 3 + d], r[name + "_q"].at[1 + slot],
                        dev_uv(axis, u, (v + d) % 4, xh),
                    ),
                    on_diag if kind else None,
                )

    def g2_arrive(name):
        axis = GATHERS[name][1]
        u, v = uv(axis)
        for p in range(5):
            arrive(r[name].at[c, u, p], r[name + "_q"].at[1 + p], v != target(axis, p))

    def g3(name):
        axis = GATHERS[name][1]
        u, v = uv(axis)
        place = r[name].at[c, u]
        for d in (1, 3, 2):
            launch(
                rcopy(
                    place, place, r[name + "_s"].at[6 + d], r[name + "_q"].at[5 + d],
                    dev_uv(axis, (u + d) % 4, v, xh),
                )
            )

    def g3_arrive(name):
        u, _ = uv(GATHERS[name][1])
        for d in (1, 2, 3):
            arrive(r[name].at[c, (u - d + 4) % 4], r[name + "_q"].at[5 + d])

    def g4(name):
        place = r[name].at[c]
        launch(rcopy(place, place, r[name + "_s"].at[10], r[name + "_q"].at[9], sibling))

    def g4_arrive(name):
        arrive(r[name].at[1 - c], r[name + "_q"].at[9])

    x1, x2, x2o = r["x1"], r["x2"], r["x2o"]

    def part_head(p, j):
        half = (1 - c) if j < 4 else c
        return half, j % 4, half * HALF + head_of(j % 4, p)

    def columns(h):
        return pl.ds(pl.multiple_of(h * HD, HD), HD)

    def exchange(lo, hi):
        for n in range(lo, hi):
            p, j = n // 8, n % 8
            _, _, h = part_head(p, j)
            src = r["x2_hbm"].at[0, :, columns(h)] if n < FROM_HBM else x2.at[:, columns(h)]
            sem = 2 * p + j // 4
            rcopy(src, x2o.at[p, j], r["x_s"].at[sem], r["x_q"].at[sem], twin).start()

    load1 = pltpu.make_async_copy(r["x1_hbm"].at[0], x1, r["l_s"].at[0])
    load2 = pltpu.make_async_copy(r["x2_hbm"].at[0], x2, r["l_s"].at[1])
    load2.start()
    load1.start()
    barrier = pltpu.get_barrier_semaphore()
    peers = [sibling, twin]
    for i in range(1, 8):
        peers.append(dev(z, (y + i // 2) % 4, (xh + i % 2) % 2, c))
    for i in range(2, 8):
        peers.append(dev((z + i // 2) % 4, y, (xh + i % 2) % 2, c))
    for i in range(1, 4):
        peers.append(dev((z + i) % 4, y, xh, 1 - c))
    for peer in peers:
        pl.semaphore_signal(barrier, inc=1, device_id=peer, device_id_type=MESH)
    pl.semaphore_wait(barrier, len(peers))
    exchange(0, FROM_HBM)
    load2.wait()
    exchange(FROM_HBM, BATCHES[0])
    load1.wait()

    upper, diag = masks()
    eye = jnp.where(diag, 1.0, 0.0).astype(F32)
    row8 = iota((8, HD), 0)

    def gram(h):
        ch, zz, yy, p = places(h)
        cols = columns(h)
        ab = jnp.concatenate([x1[:, cols], x2[:, cols]], axis=1)
        g = dot_t(ab, ab)
        sums = jnp.dot(jnp.ones((8, ab.shape[0]), ab.dtype), ab, preferred_element_type=F32)
        g1_, cr, g2_ = g[:HD, :HD], g[:HD, HD:], g[HD:, HD:]
        packed = jnp.where(upper, g1_, g2_)
        dg = jnp.sum(jnp.where(diag, g2_, 0.0), axis=0, keepdims=True)
        aux = jnp.where(
            row8 == 0, sums[:, :HD],
            jnp.where(row8 == 1, sums[:, HD:], jnp.where(row8 == 2, jnp.broadcast_to(dg, (8, HD)), 0.0)),
        )
        r["pa"][ch, zz, p, 0:64] = packed[:64]
        r["pa"][ch, zz, p, 64:72] = aux
        r["pb"][ch, yy, p] = packed[64:]
        r["ca"][ch, zz, p] = cr[:64]
        r["cb"][ch, yy, p] = cr[64:]

    def cross(p, which):
        arrive(x2o.at[p, pl.ds(4 * which, 4)], r["x_q"].at[2 * p + which])
        for j in range(4 * which, 4 * which + 4):
            half, zz, h = part_head(p, j)
            yy = zz if p == 4 else (zz + p) % 4
            cr = dot_t(x1[:, columns(h)], x2o[p, j])
            r["da"][p, half, zz] = cr[:64]
            r["db"][p, half, yy] = cr[64:]
            if j == 3:
                for name in LATE:
                    launch(
                        rcopy(
                            r[name].at[p, 1 - c], r[name + "_r1"].at[p], r[name + "_s"].at[p],
                            r[name + "_q"].at[p], sibling,
                        )
                    )

    def cross_s2(p):
        for name, axis in LATE.items():
            buf, r1 = r[name], r[name + "_r1"]
            u, v = uv(axis)
            arrive(r1.at[p], r[name + "_q"].at[p])
            for i in range(4):
                buf[p, c, i] = buf[p, c, i] + r1[p, i]
            for d in (1, 3, 2):
                to = (u + d) % 4
                launch(
                    rcopy(
                        buf.at[p, c, to], r[name + "_r2"].at[p, d - 1], r[name + "_s"].at[2 + 3 * (p + 1) + d - 1],
                        r[name + "_q"].at[2 + 3 * (p + 1) + d - 1], dev_uv(axis, to, v, xh),
                    )
                )

    def cross_s2_sum(p):
        for name, axis in LATE.items():
            buf, r2 = r[name], r[name + "_r2"]
            u, _ = uv(axis)
            for d in (1, 2, 3):
                arrive(r2.at[p, d - 1], r[name + "_q"].at[2 + 3 * (p + 1) + d - 1])
            r[name + "x_acc"][p] = (buf[p, c, u] + r2[p, 0]) + (r2[p, 1] + r2[p, 2])

    def last_s3():
        for name, axis in LATE.items():
            u, v = uv(axis)
            slot = ((v - u + 4) % 4) * 2 + 1 - xh
            launch(
                rcopy(
                    r[name + "x_acc"].at[4], r[name + "_r5"].at[slot], r[name + "_s"].at[20],
                    r[name + "_q"].at[20 + slot], dev_uv(axis, u, u, 1),
                ),
                no(late_owner),
            )

    def last_total(name):
        total = r[name + "x_acc"][4]
        for slot in range(1, 8):
            arrive(r[name + "_r5"].at[slot], r[name + "_q"].at[20 + slot])
        for slot in range(1, 8):
            total = total + r[name + "_r5"][slot]
        return total

    def only_row0(row):
        return jnp.where(row8 == 0, jnp.broadcast_to(row, (8, HD)), 0.0)

    def similarity(raw, sums, w2):
        mean1 = only_row0(r["aux"][0:1, :]) / tokens
        cov = raw / tokens - dot_t(mean1, only_row0(sums) / tokens, HI)
        white = mm(mm(r["w12"][0], cov), w2)
        sq = jnp.sum(jnp.sum(white * white, axis=1, keepdims=True), axis=0, keepdims=True)
        return jnp.broadcast_to(sq / HD, (8, HD))

    def whiten():
        top = s4_total("pa", True)
        low = s4_total("pb", True)
        aux = top[64:72]
        grams = unpack(top[:64], low, aux)
        ys, zs, scales = [], [], []
        for n in (0, 1):
            mean = only_row0(aux[n : n + 1, :]) / tokens
            cov = grams[n] / tokens - dot_t(mean, mean, HI) + RIDGE * eye
            sq = jnp.sum(jnp.sum(cov * cov, axis=1, keepdims=True), axis=0, keepdims=True)
            scale = jnp.sqrt(sq)
            scales.append(scale)
            ys.append(cov / scale)
        for it in range(ITERS):
            for n in (0, 1):
                if it == 0:
                    f = 1.5 * eye - 0.5 * ys[n]
                    zs.append(f)
                else:
                    f = 1.5 * eye - 0.5 * mm(zs[n], ys[n])
                    zs[n] = mm(f, zs[n])
                if it < ITERS - 1:
                    ys[n] = mm(ys[n], f)
        w1 = zs[0] / jnp.sqrt(scales[0])
        w2 = zs[1] / jnp.sqrt(scales[1])
        wp = jnp.where(upper, w1, w2)
        wd = jnp.sum(jnp.where(diag, w2, 0.0), axis=0, keepdims=True)
        r["wa"][c, z, own, 0:64] = wp[:64]
        r["wa"][c, z, own, 64:72] = jnp.broadcast_to(wd, (8, HD))
        r["wb"][c, y, own] = wp[64:]
        g1("wa")
        g1("wb")
        r["w12"][0] = w1
        r["w12"][1] = w2
        r["aux"][...] = aux
        r["w_out_x"][0:HD] = w2
        r["w_out_x"][HD : HD + 8] = aux
        rcopy(r["w_out_x"], r["w_in_x"], r["y_s"].at[0], r["y_q"].at[0], twin).start()

    def both(p):
        cross(p, 0)
        cross(p, 1)

    loop(HALF, lambda i: gram((1 - c) * HALF + i), unroll=2)
    for name in CHAINS:
        s1(name)
    loop(HALF, lambda i: gram(c * HALF + i), unroll=2)
    for name in ("pa", "pb"):
        s1_sum(name)
        s2(name)
    for name in ("ca", "cb"):
        s1_sum(name)
    both(0)
    for name in ("pa", "pb"):
        s2_sum(name)
        s3(name, CHAINS[name][1], range(5))
    for name in ("pa", "pb"):
        s3_sum(name, True)
        s4(name, True)
    exchange(BATCHES[0], BATCHES[1])
    for name in ("ca", "cb"):
        s2(name)
    pl.when(owner)(whiten)
    exchange(BATCHES[1], BATCHES[2])
    for name in GATHERS:
        g1_arrive(name)
        g2(name)
    both(1)
    cross_s2(0)
    for name in ("ca", "cb"):
        s2_sum(name)
        s3(name, CHAINS[name][1], range(5))
    for name in GATHERS:
        g2_arrive(name)
        g3(name)
    for name in ("ca", "cb"):
        s3_sum(name, True)
        s4(name, True)
    exchange(BATCHES[2], 8 * PARTS)
    cross_s2(1)
    both(2)
    cross_s2_sum(0)

    lane_head = c * HALF + jnp.where(own == 4, 16 + z, head_of(z, own))
    here = iota((8, HD), 1) == lane_head
    sa_mine = r["sa"].at[c, z, own]

    def own_similarity():
        raw = jnp.concatenate([s4_total("ca", True), s4_total("cb", True)], axis=0)
        sim = similarity(raw, r["aux"][1:2, :], r["w12"][1])
        sa_mine[...] = jnp.where(jnp.logical_and(here, row8 == lay), sim, 0.0)
        arrive(r["w_in_x"], r["y_q"].at[0])

    def other_similarity(raw):
        sim = similarity(raw, r["w_in_x"][HD + 1 : HD + 2], r["w_in_x"][0:HD])
        sa_mine[...] = jnp.where(jnp.logical_and(here, row8 == 1 - lay), sim, sa_mine[...])
        for i in range(1, 8):
            rcopy(
                sa_mine, sa_mine, r["sa_s"].at[i], r["sa_q"].at[own],
                dev(z, (y + i // 2) % 4, (xh + i % 2) % 2, c),
            ).start()

    def emit(h):
        ch, zz, yy, p = places(h)
        w1, w2 = unpack(r["wa"][ch, zz, p, 0:64], r["wb"][ch, yy, p], r["wa"][ch, zz, p, 64:72])
        r["w"][0, h] = w1
        r["w"][1, h] = w2

    pl.when(owner)(own_similarity)
    cross_s2(2)
    cross_s2_sum(1)
    for name in GATHERS:
        g3_arrive(name)
        g4(name)
    both(3)
    cross_s2_sum(2)
    cross_s2(3)
    for name in GATHERS:
        g4_arrive(name)
    loop(HEADS, emit, unroll=2)
    cross_s2_sum(3)
    for name, axis in LATE.items():
        s3(name + "x", axis, range(4))
    for name in LATE:
        s3_sum(name + "x", False)
        s4(name + "x", False)
    cross(4, 0)
    cross(4, 1)
    cross_s2(4)
    cross_s2_sum(4)
    last_s3()

    @pl.when(early_owner)
    def _():
        other_similarity(jnp.concatenate([s4_total("dax", False), s4_total("dbx", False)], axis=0))

    @pl.when(late_owner)
    def _():
        other_similarity(jnp.concatenate([last_total("da"), last_total("db")], axis=0))

    for p in range(5):
        arrive(r["sa"].at[c, z, p], r["sa_q"].at[p], no(jnp.logical_and(owner, own == p)))
    mine = r["sa"].at[c, z]
    for i in range(1, 8):
        launch(
            rcopy(
                mine, mine, r["sa_s"].at[7 + i], r["sa_q"].at[4 + i],
                dev((z + i // 2) % 4, y, xh, (c + i % 2) % 2),
            )
        )
    for i in range(1, 8):
        arrive(r["sa"].at[(c + i % 2) % 2, (z - i // 2 + 4) % 4], r["sa_q"].at[4 + i])

    total = jnp.zeros((8, HD), F32)
    for ch in range(2):
        for i in range(4):
            for s in range(5):
                total = total + r["sa"][ch, i, s]
    r["sim"][...] = total

    for cond, copy in pending:
        if cond is None:
            copy.wait_send()
        else:
            pl.when(cond)(lambda copy=copy: copy.wait_send())
    for i in range(2 * PARTS):
        part = x2o.at[i // 2, pl.ds(4 * (i % 2), 4)]
        rcopy(part, part, r["x_s"].at[i], r["x_q"].at[i], twin).wait_send()

    @pl.when(owner)
    def _():
        for name in GATHERS:
            u, _ = uv(GATHERS[name][1])
            place = r[name].at[c, u, own]
            rcopy(place, place, r[name + "_s"].at[0], r[name + "_q"].at[0], far).wait_send()
        rcopy(r["w_out_x"], r["w_in_x"], r["y_s"].at[0], r["y_q"].at[0], twin).wait_send()
        for i in range(1, 8):
            rcopy(sa_mine, sa_mine, r["sa_s"].at[i], r["sa_q"].at[own], far).wait_send()


def gather_kernel(tokens, first_acts, second_acts):
    rows, width = first_acts.shape[1:]
    names = ["x1_hbm", "x2_hbm", "w", "sim"]
    scratch = []

    def add(name, spec):
        names.append(name)
        scratch.append(spec)

    dma = lambda n: pltpu.SemaphoreType.DMA((n,))
    for name in ("x1", "x2"):
        add(name, pltpu.VMEM((rows, width), first_acts.dtype))
    add("x2o", pltpu.VMEM((PARTS, 8, rows, HD), first_acts.dtype))
    for name, (n, _) in CHAINS.items():
        add(name, pltpu.VMEM((2, 4, 5, n, HD), F32))
        add(name + "_r1", pltpu.VMEM((4, 5, n, HD), F32))
        add(name + "_r2", pltpu.VMEM((3, 5, n, HD), F32))
    for name in LATE:
        add(name, pltpu.VMEM((PARTS, 2, 4, 64, HD), F32))
        add(name + "_r1", pltpu.VMEM((PARTS, 4, 64, HD), F32))
        add(name + "_r2", pltpu.VMEM((PARTS, 3, 64, HD), F32))
        add(name + "_r5", pltpu.VMEM((8, 64, HD), F32))
        add(name + "_s", dma(21))
        add(name + "_q", dma(28))
    for name, n in [(k, v[0]) for k, v in CHAINS.items()] + [(k + "x", 64) for k in LATE]:
        add(name + "_acc", pltpu.VMEM((5, n, HD), F32))
        add(name + "_r3", pltpu.VMEM((2, 3, n, HD), F32))
        add(name + "_t", pltpu.VMEM((2, n, HD), F32))
        add(name + "_r4", pltpu.VMEM((n, HD), F32))
        add(name + "_s", dma(10))
        add(name + "_q", dma(11))
    add("sa", pltpu.VMEM((2, 4, 5, 8, HD), F32))
    for name, (n, _) in GATHERS.items():
        add(name, pltpu.VMEM((2, 4, 5, n, HD), F32))
        add(name + "_s", dma(11))
        add(name + "_q", dma(10))
    add("sa_s", dma(15))
    add("sa_q", dma(12))
    add("w12", pltpu.VMEM((2, HD, HD), F32))
    add("aux", pltpu.VMEM((8, HD), F32))
    add("w_out_x", pltpu.VMEM((HD + 8, HD), F32))
    add("w_in_x", pltpu.VMEM((HD + 8, HD), F32))
    add("l_s", dma(2))
    add("x_s", dma(2 * PARTS))
    add("x_q", dma(2 * PARTS))
    add("y_s", dma(1))
    add("y_q", dma(1))
    add("none", dma(1))
    return pl.pallas_call(
        functools.partial(kernel, tokens, names),
        out_shape=(
            pltpu.VMEM((2, HEADS, HD, HD), F32),
            pltpu.VMEM((8, HD), F32),
        ),
        in_specs=[pl.BlockSpec(memory_space=pltpu.HBM)] * 2,
        out_specs=[pl.BlockSpec(memory_space=pltpu.VMEM)] * 2,
        scratch_shapes=scratch,
        compiler_params=pltpu.CompilerParams(
            collective_id=0, has_side_effects=True, vmem_limit_bytes=VMEM_LIMIT
        ),
    )(
        pltpu.with_memory_space_constraint(first_acts, pltpu.HBM),
        pltpu.with_memory_space_constraint(second_acts, pltpu.HBM),
    )


def store_kernel(w, sim, w_hbm, s_ref, sem):
    copy = pltpu.make_async_copy(w, w_hbm.at[:, 0], sem.at[0])
    copy.start()
    s_ref[0] = sim[0:2, 0:HEADS]
    copy.wait()


def store(w, sim):
    vmem = pl.BlockSpec(memory_space=pltpu.VMEM)
    return pl.pallas_call(
        store_kernel,
        out_shape=(
            jax.ShapeDtypeStruct((2, 1, HEADS, HD, HD), F32),
            jax.ShapeDtypeStruct((1, 2, HEADS), F32),
        ),
        in_specs=[vmem] * 2,
        out_specs=(pl.BlockSpec(memory_space=pltpu.HBM), vmem),
        scratch_shapes=[pltpu.SemaphoreType.DMA((1,))],
        compiler_params=pltpu.CompilerParams(vmem_limit_bytes=16 * 2**20),
    )(w, sim)


def solution(mesh):
    def whole(first_acts, second_acts):
        tokens = first_acts.shape[1] * lax.axis_size("tok")
        return store(*gather_kernel(tokens, first_acts, second_acts))

    in_specs = (P("lay", "tok", None), P("lay", "tok", None))
    out_specs = (P(None, "lay", None, None, None), P("lay", None, None))
    return jax.shard_map(whole, mesh=mesh, in_specs=in_specs, out_specs=out_specs, check_vma=False)
```

time: 988 us -> 98.9 us (0.10)
  waiting for transfers between devices: 792 us -> 0 us
  matrix products: 144 us -> 0 us
  Pallas kernels: 0 us -> 98.1 us
  other arithmetic: 14.5 us -> 0 us
  between operations: 14.5 us -> 0.64 us
  local copies, waits for them, and re-layouts: 13.8 us -> 0 us
    psum x1 -> x0, waiting for transfers between devices: 668 us -> none  [in_one(): total = lax.psum(line, axis)]
    dot_general x22 -> x0, matrix products: 144 us -> none  [the longest x6 42 us: newton_whiten(): jnp.matmul(factor_iter, inverse_iter, precision=top_precision)]
    all_gather x2 -> x0, waiting for transfers between devices: 123 us -> none  [the longest x1 65.3 us: local(): gathered = lax.all_gather(second_acts, 'lay', axis=0, tiled=True)]
    pallas_call x0 -> x2, Pallas kernels: none -> 98.1 us  [the longest x1 95.2 us: gather_kernel(): pl.pallas_call(functools.partial(kernel, tokens, names), out_shape=(pltpu...]
  transfers between devices with their start and end apart: 3 -> 0, of which waited for: 3 -> 0; matrix products, arithmetic and copies ran while one was open for 2% -> 0% of each run, Pallas kernels for 0% -> 0%
where the time goes in v2:
time: 98.9 us; the launch traced here: 98.8 us
  Pallas kernels  98.1 us (99%)
    pallas_call x1, Pallas kernels, gather_kernel(): pl.pallas_call(functools.partial(kernel, tokens, names), out_shape=(pltpu...  95.2 us
    pallas_call x1, Pallas kernels, store(): pl.pallas_call(store_kernel, out_shape=(jax.ShapeDtypeStruct((2, 1, HEADS...  2.93 us

profile of v2, /device:TPU:1, one launch (start us, length us, event | category | flops | bytes accessed | tf_op | source)
XLA Modules:
  0.0 98.8 jit_solution(14356065100443024790)
XLA Ops:
  0.6 95.2 %shard_map.41 = (f32[2,40,128,128]{3,2,1,0:T(8,128)S(1)}, f32[8,128]{1,0:T(8,128)S(1)}) custom-call(bf16[1,256,5120]{2,1,0:T(8,128)(2,1)} %refs_0_.1, bf16[1,256,5120]{2,1,0:T(8,128)(2,1)} %refs_1_.1), custom_call_target="tpu_custom_call" | custom-call | tf_op jit(solution)/shard_map/pallas_call | solution.py:622
  95.8 2.9 %shard_map.42 = (f32[2,1,40,128,128]{4,3,2,1,0:T(8,128)}, f32[1,2,40]{2,1,0:T(2,128)}) custom-call(f32[2,40,128,128]{3,2,1,0:T(8,128)S(1)} %get-tuple-element.4.w, f32[8,128]{1,0:T(8,128)S(1)} %get-tuple-element.5.sim), custom_call_target="tpu_custom_call" | custom-call | tf_op jit(solution)/shard_map/pallas_call | solution.py:649

commit v3 on v2

--- a/solution.py
+++ b/solution.py
@@ -114,6 +114,7 @@
             device_id=device, device_id_type=MESH,
         )
 
+    others = lax.axis_size("tok") - 1
     pending = []
 
     def launch(copy, cond=None):
@@ -287,8 +288,6 @@
         peers.append(dev(z, (y + i // 2) % 4, (xh + i % 2) % 2, c))
     for i in range(2, 8):
         peers.append(dev((z + i // 2) % 4, y, (xh + i % 2) % 2, c))
-    for i in range(1, 4):
-        peers.append(dev((z + i) % 4, y, xh, 1 - c))
     for peer in peers:
         pl.semaphore_signal(barrier, inc=1, device_id=peer, device_id_type=MESH)
     pl.semaphore_wait(barrier, len(peers))
@@ -476,7 +475,7 @@
 
     lane_head = c * HALF + jnp.where(own == 4, 16 + z, head_of(z, own))
     here = iota((8, HD), 1) == lane_head
-    sa_mine = r["sa"].at[c, z, own]
+    sa_mine = r["sa"].at[(c * 4 + z) * 5 + own]
 
     def own_similarity():
         raw = jnp.concatenate([s4_total("ca", True), s4_total("cb", True)], axis=0)
@@ -487,11 +486,13 @@
     def other_similarity(raw):
         sim = similarity(raw, r["w_in_x"][HD + 1 : HD + 2], r["w_in_x"][0:HD])
         sa_mine[...] = jnp.where(jnp.logical_and(here, row8 == 1 - lay), sim, sa_mine[...])
-        for i in range(1, 8):
-            rcopy(
-                sa_mine, sa_mine, r["sa_s"].at[i], r["sa_q"].at[own],
-                dev(z, (y + i // 2) % 4, (xh + i % 2) % 2, c),
-            ).start()
+
+        def send(t):
+            @pl.when(t != tok)
+            def _():
+                rcopy(sa_mine, sa_mine, r["sa_s"].at[0], r["sa_q"].at[0], (t, lay)).start()
+
+        loop(lax.axis_size("tok"), send)
 
     def emit(h):
         ch, zz, yy, p = places(h)
@@ -514,12 +515,12 @@
     cross_s2_sum(3)
     for name, axis in LATE.items():
         s3(name + "x", axis, range(4))
+    cross(4, 0)
+    cross(4, 1)
+    cross_s2(4)
     for name in LATE:
         s3_sum(name + "x", False)
         s4(name + "x", False)
-    cross(4, 0)
-    cross(4, 1)
-    cross_s2(4)
     cross_s2_sum(4)
     last_s3()
 
@@ -531,25 +532,12 @@
     def _():
         other_similarity(jnp.concatenate([last_total("da"), last_total("db")], axis=0))
 
-    for p in range(5):
-        arrive(r["sa"].at[c, z, p], r["sa_q"].at[p], no(jnp.logical_and(owner, own == p)))
-    mine = r["sa"].at[c, z]
-    for i in range(1, 8):
-        launch(
-            rcopy(
-                mine, mine, r["sa_s"].at[7 + i], r["sa_q"].at[4 + i],
-                dev((z + i // 2) % 4, y, xh, (c + i % 2) % 2),
-            )
-        )
-    for i in range(1, 8):
-        arrive(r["sa"].at[(c + i % 2) % 2, (z - i // 2 + 4) % 4], r["sa_q"].at[4 + i])
-
-    total = jnp.zeros((8, HD), F32)
-    for ch in range(2):
-        for i in range(4):
-            for s in range(5):
-                total = total + r["sa"][ch, i, s]
-    r["sim"][...] = total
+    pl.when(owner)(lambda: arrive(r["sa"].at[pl.ds(0, HEADS - 1)], r["sa_q"].at[0]))
+    pl.when(no(owner))(lambda: arrive(r["sa"].at[pl.ds(0, HEADS)], r["sa_q"].at[0]))
+    total = r["sa"][0]
+    for i in range(1, HEADS):
+        total = total + r["sa"][i]
+    r["sim"][...] = total[0:2, 0:HEADS]
 
     for cond, copy in pending:
         if cond is None:
@@ -567,8 +555,8 @@
             place = r[name].at[c, u, own]
             rcopy(place, place, r[name + "_s"].at[0], r[name + "_q"].at[0], far).wait_send()
         rcopy(r["w_out_x"], r["w_in_x"], r["y_s"].at[0], r["y_q"].at[0], twin).wait_send()
-        for i in range(1, 8):
-            rcopy(sa_mine, sa_mine, r["sa_s"].at[i], r["sa_q"].at[own], far).wait_send()
+        sent = r["sa"].at[pl.ds(0, others)]
+        rcopy(sent, sent, r["sa_s"].at[0], r["sa_q"].at[0], far).wait_send()
 
 
 def gather_kernel(tokens, first_acts, second_acts):
@@ -602,13 +590,13 @@
         add(name + "_r4", pltpu.VMEM((n, HD), F32))
         add(name + "_s", dma(10))
         add(name + "_q", dma(11))
-    add("sa", pltpu.VMEM((2, 4, 5, 8, HD), F32))
+    add("sa", pltpu.VMEM((64, 8, HD), F32))
     for name, (n, _) in GATHERS.items():
         add(name, pltpu.VMEM((2, 4, 5, n, HD), F32))
         add(name + "_s", dma(11))
         add(name + "_q", dma(10))
-    add("sa_s", dma(15))
-    add("sa_q", dma(12))
+    add("sa_s", dma(1))
+    add("sa_q", dma(1))
     add("w12", pltpu.VMEM((2, HD, HD), F32))
     add("aux", pltpu.VMEM((8, HD), F32))
     add("w_out_x", pltpu.VMEM((HD + 8, HD), F32))
@@ -623,7 +611,7 @@
         functools.partial(kernel, tokens, names),
         out_shape=(
             pltpu.VMEM((2, HEADS, HD, HD), F32),
-            pltpu.VMEM((8, HD), F32),
+            pltpu.VMEM((2, HEADS), F32),
         ),
         in_specs=[pl.BlockSpec(memory_space=pltpu.HBM)] * 2,
         out_specs=[pl.BlockSpec(memory_space=pltpu.VMEM)] * 2,
@@ -637,15 +625,27 @@
     )
 
 
-def store_kernel(w, sim, w_hbm, s_ref, sem):
-    copy = pltpu.make_async_copy(w, w_hbm.at[:, 0], sem.at[0])
-    copy.start()
-    s_ref[0] = sim[0:2, 0:HEADS]
-    copy.wait()
+PIECES = 4
+
+
+def store_kernel(w, sim, w_hbm, s_hbm, sems):
+    step = HEADS // PIECES
+    copies = [
+        pltpu.make_async_copy(
+            w.at[n, pl.ds(q * step, step)], w_hbm.at[n, 0, pl.ds(q * step, step)], sems.at[n * PIECES + q]
+        )
+        for n in range(2)
+        for q in range(PIECES)
+    ]
+    copies.append(pltpu.make_async_copy(sim, s_hbm.at[0], sems.at[2 * PIECES]))
+    for copy in copies:
+        copy.start()
+    for copy in copies:
+        copy.wait()
 
 
 def store(w, sim):
-    vmem = pl.BlockSpec(memory_space=pltpu.VMEM)
+    vmem, hbm = pl.BlockSpec(memory_space=pltpu.VMEM), pl.BlockSpec(memory_space=pltpu.HBM)
     return pl.pallas_call(
         store_kernel,
         out_shape=(
@@ -653,8 +653,8 @@
             jax.ShapeDtypeStruct((1, 2, HEADS), F32),
         ),
         in_specs=[vmem] * 2,
-        out_specs=(pl.BlockSpec(memory_space=pltpu.HBM), vmem),
-        scratch_shapes=[pltpu.SemaphoreType.DMA((1,))],
+        out_specs=(hbm, hbm),
+        scratch_shapes=[pltpu.SemaphoreType.DMA((2 * PIECES + 1,))],
         compiler_params=pltpu.CompilerParams(vmem_limit_bytes=16 * 2**20),
     )(w, sim)
 

time: 98.9 us -> 94.4 us (0.954)
  Pallas kernels: 98.1 us -> 93.7 us
    pallas_call x1, Pallas kernels: 95.2 us -> 91.3 us  [gather_kernel(): pl.pallas_call(functools.partial(kernel, tokens, names), out_shape=(pltpu...]
where the time goes in v3:
time: 94.4 us; the launch traced here: 94.3 us
  Pallas kernels  93.7 us (99%)
    pallas_call x1, Pallas kernels, gather_kernel(): pl.pallas_call(functools.partial(kernel, tokens, names), out_shape=(pltpu...  91.3 us
    pallas_call x1, Pallas kernels, store(): pl.pallas_call(store_kernel, out_shape=(jax.ShapeDtypeStruct((2, 1, HEADS...  2.43 us

profile of v3, /device:TPU:1, one launch (start us, length us, event | category | flops | bytes accessed | tf_op | source)
XLA Modules:
  0.0 94.3 jit_solution(13961775133634926776)
XLA Ops:
  0.6 91.3 %shard_map.41 = (f32[2,40,128,128]{3,2,1,0:T(8,128)S(1)}, f32[2,40]{1,0:T(2,128)S(1)}) custom-call(bf16[1,256,5120]{2,1,0:T(8,128)(2,1)} %refs_0_.1, bf16[1,256,5120]{2,1,0:T(8,128)(2,1)} %refs_1_.1), custom_call_target="tpu_custom_call" | custom-call | tf_op jit(solution)/shard_map/pallas_call | solution.py:610
  91.9 2.4 %shard_map.42 = (f32[2,1,40,128,128]{4,3,2,1,0:T(8,128)}, f32[1,2,40]{2,1,0:T(2,128)}) custom-call(f32[2,40,128,128]{3,2,1,0:T(8,128)S(1)} %get-tuple-element.4.w, f32[2,40]{1,0:T(2,128)S(1)} %get-tuple-element.5.sim), custom_call_target="tpu_custom_call" | custom-call | tf_op jit(solution)/shard_map/pallas_call | solution.py:649

commit v4 on v3

--- a/solution.py
+++ b/solution.py
@@ -14,7 +14,7 @@
 HALF = HEADS // 2
 PARTS = 5
 FROM_HBM = 3
-BATCHES = (14, 19, 27)
+BATCHES = (14, 21, 32)
 VMEM_LIMIT = 48 * 2**20
 F32 = jnp.float32
 HI = lax.Precision.HIGHEST
@@ -267,6 +267,9 @@
         half = (1 - c) if j < 4 else c
         return half, j % 4, half * HALF + head_of(j % 4, p)
 
+    def last_head(z_, c_):
+        return c_ * HALF + 16 + z_
+
     def columns(h):
         return pl.ds(pl.multiple_of(h * HD, HD), HD)
 
@@ -275,19 +278,48 @@
             p, j = n // 8, n % 8
             _, _, h = part_head(p, j)
             src = r["x2_hbm"].at[0, :, columns(h)] if n < FROM_HBM else x2.at[:, columns(h)]
+            if p == 4:
+                src = x2.at[:, columns(last_head(z, c))] if j == 0 else r["m2"].at[j - 1]
             sem = 2 * p + j // 4
             rcopy(src, x2o.at[p, j], r["x_s"].at[sem], r["x_q"].at[sem], twin).start()
+
+    def collect():
+        for dz in (1, 3, 2, 0):
+            for dc in (0, 1):
+                j = 2 * dz + dc
+                if j:
+                    z_, c_ = (z + dz) % 4, (c + dc) % 2
+                    cols = columns(last_head(z_, c_))
+                    for n, x in ((1, x2), (0, x1)):
+                        launch(
+                            rcopy(
+                                x.at[:, cols], r["m%d" % (n + 1)].at[j - 1], r["m_s"].at[7 * n + j - 1],
+                                r["m_q"].at[7 * n + j - 1], dev(z_, y, xh, c_),
+                            )
+                        )
+
+    def collected(n):
+        for j in range(1, 8):
+            arrive(r["m%d" % (n + 1)].at[j - 1], r["m_q"].at[7 * n + j - 1])
+
+    def last_cross(which):
+        arrive(x2o.at[4, pl.ds(4 * which, 4)], r["x_q"].at[8 + which])
+        total = None
+        for j in range(4 * which, 4 * which + 4):
+            left = r["m1"][j - 1] if j else x1[:, columns(last_head(z, c))]
+            cr = dot_t(left, x2o[4, j])
+            total = cr if total is None else total + cr
+        r["d4"][...] = r["d4"][...] + total if which else total
 
     load1 = pltpu.make_async_copy(r["x1_hbm"].at[0], x1, r["l_s"].at[0])
     load2 = pltpu.make_async_copy(r["x2_hbm"].at[0], x2, r["l_s"].at[1])
     load2.start()
     load1.start()
     barrier = pltpu.get_barrier_semaphore()
-    peers = [sibling, twin]
-    for i in range(1, 8):
-        peers.append(dev(z, (y + i // 2) % 4, (xh + i % 2) % 2, c))
-    for i in range(2, 8):
-        peers.append(dev((z + i // 2) % 4, y, (xh + i % 2) % 2, c))
+    peers = [sibling, twin, far]
+    for d in range(1, 4):
+        peers.append(dev((z + d) % 4, y, xh, c))
+        peers.append(dev(z, (y + d) % 4, xh, c))
     for peer in peers:
         pl.semaphore_signal(barrier, inc=1, device_id=peer, device_id_type=MESH)
     pl.semaphore_wait(barrier, len(peers))
@@ -323,7 +355,7 @@
         arrive(x2o.at[p, pl.ds(4 * which, 4)], r["x_q"].at[2 * p + which])
         for j in range(4 * which, 4 * which + 4):
             half, zz, h = part_head(p, j)
-            yy = zz if p == 4 else (zz + p) % 4
+            yy = (zz + p) % 4
             cr = dot_t(x1[:, columns(h)], x2o[p, j])
             r["da"][p, half, zz] = cr[:64]
             r["db"][p, half, yy] = cr[64:]
@@ -361,32 +393,29 @@
             r[name + "x_acc"][p] = (buf[p, c, u] + r2[p, 0]) + (r2[p, 1] + r2[p, 2])
 
     def last_s3():
-        for name, axis in LATE.items():
-            u, v = uv(axis)
-            slot = ((v - u + 4) % 4) * 2 + 1 - xh
-            launch(
-                rcopy(
-                    r[name + "x_acc"].at[4], r[name + "_r5"].at[slot], r[name + "_s"].at[20],
-                    r[name + "_q"].at[20 + slot], dev_uv(axis, u, u, 1),
-                ),
-                no(late_owner),
-            )
-
-    def last_total(name):
-        total = r[name + "x_acc"][4]
+        slot = ((y - z + 4) % 4) * 2 + 1 - xh
+        launch(
+            rcopy(r["d4"], r["r5"].at[slot], r["d4_s"].at[0], r["d4_q"].at[slot], dev(z, z, 1, c)),
+            no(late_owner),
+        )
+
+    def last_total():
         for slot in range(1, 8):
-            arrive(r[name + "_r5"].at[slot], r[name + "_q"].at[20 + slot])
-        for slot in range(1, 8):
-            total = total + r[name + "_r5"][slot]
+            arrive(r["r5"].at[slot], r["d4_q"].at[slot])
+        total = r["d4"][...] + r["r5"][1]
+        for slot in range(2, 8):
+            total = total + r["r5"][slot]
         return total
 
     def only_row0(row):
         return jnp.where(row8 == 0, jnp.broadcast_to(row, (8, HD)), 0.0)
 
-    def similarity(raw, sums, w2):
+    def mean_term(sums):
         mean1 = only_row0(r["aux"][0:1, :]) / tokens
-        cov = raw / tokens - dot_t(mean1, only_row0(sums) / tokens, HI)
-        white = mm(mm(r["w12"][0], cov), w2)
+        return dot_t(mean1, only_row0(sums) / tokens, HI)
+
+    def similarity(raw, means, w2):
+        white = mm(mm(r["w12"][0], raw / tokens - means), w2)
         sq = jnp.sum(jnp.sum(white * white, axis=1, keepdims=True), axis=0, keepdims=True)
         return jnp.broadcast_to(sq / HD, (8, HD))
 
@@ -427,8 +456,6 @@
         r["aux"][...] = aux
         r["w_out_x"][0:HD] = w2
         r["w_out_x"][HD : HD + 8] = aux
-        rcopy(r["w_out_x"], r["w_in_x"], r["y_s"].at[0], r["y_q"].at[0], twin).start()
-
     def both(p):
         cross(p, 0)
         cross(p, 1)
@@ -446,6 +473,7 @@
     for name in ("pa", "pb"):
         s2_sum(name)
         s3(name, CHAINS[name][1], range(5))
+    collect()
     for name in ("pa", "pb"):
         s3_sum(name, True)
         s4(name, True)
@@ -465,10 +493,16 @@
     for name in GATHERS:
         g2_arrive(name)
         g3(name)
+    collected(1)
+    exchange(BATCHES[2], 8 * PARTS)
     for name in ("ca", "cb"):
         s3_sum(name, True)
         s4(name, True)
-    exchange(BATCHES[2], 8 * PARTS)
+
+    @pl.when(owner)
+    def _():
+        rcopy(r["w_out_x"], r["w_in_x"], r["y_s"].at[0], r["y_q"].at[0], twin).start()
+
     cross_s2(1)
     both(2)
     cross_s2_sum(0)
@@ -479,20 +513,20 @@
 
     def own_similarity():
         raw = jnp.concatenate([s4_total("ca", True), s4_total("cb", True)], axis=0)
-        sim = similarity(raw, r["aux"][1:2, :], r["w12"][1])
+        sim = similarity(raw, mean_term(r["aux"][1:2, :]), r["w12"][1])
         sa_mine[...] = jnp.where(jnp.logical_and(here, row8 == lay), sim, 0.0)
         arrive(r["w_in_x"], r["y_q"].at[0])
+        r["means"][...] = mean_term(r["w_in_x"][HD + 1 : HD + 2])
 
     def other_similarity(raw):
-        sim = similarity(raw, r["w_in_x"][HD + 1 : HD + 2], r["w_in_x"][0:HD])
+        sim = similarity(raw, r["means"][...], r["w_in_x"][0:HD])
         sa_mine[...] = jnp.where(jnp.logical_and(here, row8 == 1 - lay), sim, sa_mine[...])
 
-        def send(t):
-            @pl.when(t != tok)
-            def _():
-                rcopy(sa_mine, sa_mine, r["sa_s"].at[0], r["sa_q"].at[0], (t, lay)).start()
-
-        loop(lax.axis_size("tok"), send)
+        def send(i):
+            to = (tok + 1 + (25 + i) % others) % (others + 1)
+            rcopy(sa_mine, sa_mine, r["sa_s"].at[0], r["sa_q"].at[0], (to, lay)).start()
+
+        loop(others, send, unroll=9)
 
     def emit(h):
         ch, zz, yy, p = places(h)
@@ -500,7 +534,6 @@
         r["w"][0, h] = w1
         r["w"][1, h] = w2
 
-    pl.when(owner)(own_similarity)
     cross_s2(2)
     cross_s2_sum(1)
     for name in GATHERS:
@@ -515,14 +548,14 @@
     cross_s2_sum(3)
     for name, axis in LATE.items():
         s3(name + "x", axis, range(4))
-    cross(4, 0)
-    cross(4, 1)
-    cross_s2(4)
+    collected(0)
+    last_cross(0)
+    last_cross(1)
+    last_s3()
     for name in LATE:
         s3_sum(name + "x", False)
         s4(name + "x", False)
-    cross_s2_sum(4)
-    last_s3()
+    pl.when(owner)(own_similarity)
 
     @pl.when(early_owner)
     def _():
@@ -530,7 +563,7 @@
 
     @pl.when(late_owner)
     def _():
-        other_similarity(jnp.concatenate([last_total("da"), last_total("db")], axis=0))
+        other_similarity(last_total())
 
     pl.when(owner)(lambda: arrive(r["sa"].at[pl.ds(0, HEADS - 1)], r["sa_q"].at[0]))
     pl.when(no(owner))(lambda: arrive(r["sa"].at[pl.ds(0, HEADS)], r["sa_q"].at[0]))
@@ -577,12 +610,20 @@
         add(name + "_r1", pltpu.VMEM((4, 5, n, HD), F32))
         add(name + "_r2", pltpu.VMEM((3, 5, n, HD), F32))
     for name in LATE:
-        add(name, pltpu.VMEM((PARTS, 2, 4, 64, HD), F32))
-        add(name + "_r1", pltpu.VMEM((PARTS, 4, 64, HD), F32))
-        add(name + "_r2", pltpu.VMEM((PARTS, 3, 64, HD), F32))
-        add(name + "_r5", pltpu.VMEM((8, 64, HD), F32))
-        add(name + "_s", dma(21))
-        add(name + "_q", dma(28))
+        add(name, pltpu.VMEM((PARTS - 1, 2, 4, 64, HD), F32))
+        add(name + "_r1", pltpu.VMEM((PARTS - 1, 4, 64, HD), F32))
+        add(name + "_r2", pltpu.VMEM((PARTS - 1, 3, 64, HD), F32))
+        add(name + "_s", dma(17))
+        add(name + "_q", dma(17))
+    for name in ("m1", "m2"):
+        add(name, pltpu.VMEM((7, rows, HD), first_acts.dtype))
+    add("m_s", dma(14))
+    add("m_q", dma(14))
+    add("d4", pltpu.VMEM((HD, HD), F32))
+    add("r5", pltpu.VMEM((8, HD, HD), F32))
+    add("d4_s", dma(1))
+    add("d4_q", dma(8))
+    add("means", pltpu.VMEM((HD, HD), F32))
     for name, n in [(k, v[0]) for k, v in CHAINS.items()] + [(k + "x", 64) for k in LATE]:
         add(name + "_acc", pltpu.VMEM((5, n, HD), F32))
         add(name + "_r3", pltpu.VMEM((2, 3, n, HD), F32))

time: 94.4 us -> 93.1 us (0.986)
  Pallas kernels: 93.7 us -> 92.4 us
    pallas_call x1, Pallas kernels: 91.3 us -> 90 us  [gather_kernel(): pl.pallas_call(functools.partial(kernel, tokens, names), out_shape=(pltpu...]
where the time goes in v4:
time: 93.1 us; the launch traced here: 93 us
  Pallas kernels  92.4 us (99%)
    pallas_call x1, Pallas kernels, gather_kernel(): pl.pallas_call(functools.partial(kernel, tokens, names), out_shape=(pltpu...  90 us
    pallas_call x1, Pallas kernels, store(): pl.pallas_call(store_kernel, out_shape=(jax.ShapeDtypeStruct((2, 1, HEADS...  2.43 us

profile of v4, /device:TPU:1, one launch (start us, length us, event | category | flops | bytes accessed | tf_op | source)
XLA Modules:
  0.0 93.0 jit_solution(8769892831862349500)
XLA Ops:
  0.6 90.0 %shard_map.41 = (f32[2,40,128,128]{3,2,1,0:T(8,128)S(1)}, f32[2,40]{1,0:T(2,128)S(1)}) custom-call(bf16[1,256,5120]{2,1,0:T(8,128)(2,1)} %refs_0_.1, bf16[1,256,5120]{2,1,0:T(8,128)(2,1)} %refs_1_.1), custom_call_target="tpu_custom_call" | custom-call | tf_op jit(solution)/shard_map/pallas_call | solution.py:651
  90.6 2.4 %shard_map.42 = (f32[2,1,40,128,128]{4,3,2,1,0:T(8,128)}, f32[1,2,40]{2,1,0:T(2,128)}) custom-call(f32[2,40,128,128]{3,2,1,0:T(8,128)S(1)} %get-tuple-element.4.w, f32[2,40]{1,0:T(2,128)S(1)} %get-tuple-element.5.sim), custom_call_target="tpu_custom_call" | custom-call | tf_op jit(solution)/shard_map/pallas_call | solution.py:690

commit v5 on v4

--- a/solution.py
+++ b/solution.py
@@ -151,10 +151,10 @@
 
         loop(4, body)
 
-    def s2(name):
+    def s2(name, offsets=(1, 3, 2)):
         axis = CHAINS[name][1]
         u, v = uv(axis)
-        for d in (1, 3, 2):
+        for d in offsets:
             to = (u + d) % 4
             launch(
                 rcopy(
@@ -267,6 +267,8 @@
         half = (1 - c) if j < 4 else c
         return half, j % 4, half * HALF + head_of(j % 4, p)
 
+    own_last = jnp.where(c == 0, z, y)
+
     def last_head(z_, c_):
         return c_ * HALF + 16 + z_
 
@@ -279,24 +281,27 @@
             _, _, h = part_head(p, j)
             src = r["x2_hbm"].at[0, :, columns(h)] if n < FROM_HBM else x2.at[:, columns(h)]
             if p == 4:
-                src = x2.at[:, columns(last_head(z, c))] if j == 0 else r["m2"].at[j - 1]
+                src = x2.at[:, columns(last_head(own_last, c))] if j == 0 else r["m2"].at[j - 1]
             sem = 2 * p + j // 4
             rcopy(src, x2o.at[p, j], r["x_s"].at[sem], r["x_q"].at[sem], twin).start()
 
     def collect():
-        for dz in (1, 3, 2, 0):
-            for dc in (0, 1):
-                j = 2 * dz + dc
-                if j:
-                    z_, c_ = (z + dz) % 4, (c + dc) % 2
-                    cols = columns(last_head(z_, c_))
-                    for n, x in ((1, x2), (0, x1)):
-                        launch(
-                            rcopy(
-                                x.at[:, cols], r["m%d" % (n + 1)].at[j - 1], r["m_s"].at[7 * n + j - 1],
-                                r["m_q"].at[7 * n + j - 1], dev(z_, y, xh, c_),
-                            )
-                        )
+        for d in (1, 3, 2, 0):
+            for c_ in (0, 1):
+                if c_ == 0:
+                    w_, to, other = (z + d) % 4, dev((z + d) % 4, y, xh, 0), c
+                else:
+                    w_, to, other = (y + d) % 4, dev(z, (y + d) % 4, xh, 1), 1 - c
+                slot = jnp.maximum(2 * d + other, 1) - 1
+                cols = columns(last_head(w_, c_))
+                for n, x in ((1, x2), (0, x1)):
+                    launch(
+                        rcopy(
+                            x.at[:, cols], r["m%d" % (n + 1)].at[slot], r["m_s"].at[8 * n + 2 * d + c_],
+                            r["m_q"].at[7 * n + slot], to,
+                        ),
+                        None if d else other == 1,
+                    )
 
     def collected(n):
         for j in range(1, 8):
@@ -306,7 +311,7 @@
         arrive(x2o.at[4, pl.ds(4 * which, 4)], r["x_q"].at[8 + which])
         total = None
         for j in range(4 * which, 4 * which + 4):
-            left = r["m1"][j - 1] if j else x1[:, columns(last_head(z, c))]
+            left = r["m1"][j - 1] if j else x1[:, columns(last_head(own_last, c))]
             cr = dot_t(left, x2o[4, j])
             total = cr if total is None else total + cr
         r["d4"][...] = r["d4"][...] + total if which else total
@@ -318,8 +323,9 @@
     barrier = pltpu.get_barrier_semaphore()
     peers = [sibling, twin, far]
     for d in range(1, 4):
-        peers.append(dev((z + d) % 4, y, xh, c))
-        peers.append(dev(z, (y + d) % 4, xh, c))
+        for c_ in (c, 1 - c):
+            peers.append(dev((z + d) % 4, y, xh, c_))
+            peers.append(dev(z, (y + d) % 4, xh, c_))
     for peer in peers:
         pl.semaphore_signal(barrier, inc=1, device_id=peer, device_id_type=MESH)
     pl.semaphore_wait(barrier, len(peers))
@@ -327,6 +333,7 @@
     load2.wait()
     exchange(FROM_HBM, BATCHES[0])
     load1.wait()
+    collect()
 
     upper, diag = masks()
     eye = jnp.where(diag, 1.0, 0.0).astype(F32)
@@ -393,9 +400,13 @@
             r[name + "x_acc"][p] = (buf[p, c, u] + r2[p, 0]) + (r2[p, 1] + r2[p, 2])
 
     def last_s3():
-        slot = ((y - z + 4) % 4) * 2 + 1 - xh
+        away = jnp.where(c == 0, y - z + 4, z - y + 4) % 4
+        slot = away * 2 + 1 - xh
         launch(
-            rcopy(r["d4"], r["r5"].at[slot], r["d4_s"].at[0], r["d4_q"].at[slot], dev(z, z, 1, c)),
+            rcopy(
+                r["d4"], r["r5"].at[slot], r["d4_s"].at[0], r["d4_q"].at[slot],
+                dev(own_last, own_last, 1, c),
+            ),
             no(late_owner),
         )
 
@@ -473,20 +484,20 @@
     for name in ("pa", "pb"):
         s2_sum(name)
         s3(name, CHAINS[name][1], range(5))
-    collect()
     for name in ("pa", "pb"):
         s3_sum(name, True)
         s4(name, True)
     exchange(BATCHES[0], BATCHES[1])
     for name in ("ca", "cb"):
         s2(name)
+    cross_s2(0)
     pl.when(owner)(whiten)
     exchange(BATCHES[1], BATCHES[2])
     for name in GATHERS:
         g1_arrive(name)
         g2(name)
     both(1)
-    cross_s2(0)
+    cross_s2(1)
     for name in ("ca", "cb"):
         s2_sum(name)
         s3(name, CHAINS[name][1], range(5))
@@ -495,17 +506,15 @@
         g3(name)
     collected(1)
     exchange(BATCHES[2], 8 * PARTS)
-    for name in ("ca", "cb"):
-        s3_sum(name, True)
-        s4(name, True)
 
     @pl.when(owner)
     def _():
         rcopy(r["w_out_x"], r["w_in_x"], r["y_s"].at[0], r["y_q"].at[0], twin).start()
 
-    cross_s2(1)
     both(2)
+    cross_s2(2)
     cross_s2_sum(0)
+    cross_s2_sum(1)
 
     lane_head = c * HALF + jnp.where(own == 4, 16 + z, head_of(z, own))
     here = iota((8, HD), 1) == lane_head
@@ -534,20 +543,23 @@
         r["w"][0, h] = w1
         r["w"][1, h] = w2
 
-    cross_s2(2)
-    cross_s2_sum(1)
+    both(3)
     for name in GATHERS:
         g3_arrive(name)
         g4(name)
-    both(3)
+    cross_s2(3)
     cross_s2_sum(2)
-    cross_s2(3)
+    for name, axis in LATE.items():
+        s3(name + "x", axis, range(3))
+    for name in ("ca", "cb"):
+        s3_sum(name, True)
+        s4(name, True)
     for name in GATHERS:
         g4_arrive(name)
     loop(HEADS, emit, unroll=2)
     cross_s2_sum(3)
     for name, axis in LATE.items():
-        s3(name + "x", axis, range(4))
+        s3(name + "x", axis, (3,))
     collected(0)
     last_cross(0)
     last_cross(1)
@@ -617,7 +629,7 @@
         add(name + "_q", dma(17))
     for name in ("m1", "m2"):
         add(name, pltpu.VMEM((7, rows, HD), first_acts.dtype))
-    add("m_s", dma(14))
+    add("m_s", dma(16))
     add("m_q", dma(14))
     add("d4", pltpu.VMEM((HD, HD), F32))
     add("r5", pltpu.VMEM((8, HD, HD), F32))

time: 93.1 us -> 88.7 us (0.953)
  Pallas kernels: 92.4 us -> 88 us
    pallas_call x1, Pallas kernels: 90 us -> 85.6 us  [gather_kernel(): pl.pallas_call(functools.partial(kernel, tokens, names), out_shape=(pltpu...]
where the time goes in v5:
time: 88.7 us; the launch traced here: 88.6 us
  Pallas kernels  88 us (99%)
    pallas_call x1, Pallas kernels, gather_kernel(): pl.pallas_call(functools.partial(kernel, tokens, names), out_shape=(pltpu...  85.6 us
    pallas_call x1, Pallas kernels, store(): pl.pallas_call(store_kernel, out_shape=(jax.ShapeDtypeStruct((2, 1, HEADS...  2.43 us

profile of v5, /device:TPU:1, one launch (start us, length us, event | category | flops | bytes accessed | tf_op | source)
XLA Modules:
  0.0 88.6 jit_solution(14207107821188180859)
XLA Ops:
  0.6 85.6 %shard_map.41 = (f32[2,40,128,128]{3,2,1,0:T(8,128)S(1)}, f32[2,40]{1,0:T(2,128)S(1)}) custom-call(bf16[1,256,5120]{2,1,0:T(8,128)(2,1)} %refs_0_.1, bf16[1,256,5120]{2,1,0:T(8,128)(2,1)} %refs_1_.1), custom_call_target="tpu_custom_call" | custom-call | tf_op jit(solution)/shard_map/pallas_call | solution.py:663
  86.2 2.4 %shard_map.42 = (f32[2,1,40,128,128]{4,3,2,1,0:T(8,128)}, f32[1,2,40]{2,1,0:T(2,128)}) custom-call(f32[2,40,128,128]{3,2,1,0:T(8,128)S(1)} %get-tuple-element.4.w, f32[2,40]{1,0:T(2,128)S(1)} %get-tuple-element.5.sim), custom_call_target="tpu_custom_call" | custom-call | tf_op jit(solution)/shard_map/pallas_call | solution.py:702

commit v6 on v5

--- a/solution.py
+++ b/solution.py
@@ -63,9 +63,10 @@
 def places(h):
     k = h % HALF
     z = k % 4
-    y = jnp.where(k < 16, k // 4, z)
+    half = h // HALF
+    y = jnp.where(k < 16, k // 4, (z + 2 * half) % 4)
     p = jnp.where(k < 16, (k // 4 - z + 4) % 4, 4)
-    return h // HALF, z, y, p
+    return half, z, y, p
 
 
 def kernel(tokens, names, *refs):
@@ -90,7 +91,7 @@
     twin = (tok, 1 - lay)
     far = dev(z, y, 1 - xh, c)
 
-    on_diag = z == y
+    on_diag = y == (z + 2 * c) % 4
     main = (y - z + 4) % 4
     owns_main = xh == main % 2
     owner = jnp.logical_or(owns_main, on_diag)
@@ -105,7 +106,7 @@
     def target(axis, p):
         u, _ = uv(axis)
         if p == 4:
-            return u
+            return (u + 2 * c) % 4
         return (u + p) % 4 if axis == "z" else (u - p + 4) % 4
 
     def rcopy(src, dst, ssem, rsem, device):
@@ -123,6 +124,13 @@
             copy.start()
         else:
             pl.when(cond)(lambda: copy.start())
+
+    def drain(copies):
+        for cond, copy in copies:
+            if cond is None:
+                copy.wait_send()
+            else:
+                pl.when(cond)(lambda copy=copy: copy.wait_send())
 
     def arrive(ref, sem, cond=None):
         copy = rcopy(ref, ref, r["none"].at[0], sem, twin)
@@ -267,7 +275,7 @@
         half = (1 - c) if j < 4 else c
         return half, j % 4, half * HALF + head_of(j % 4, p)
 
-    own_last = jnp.where(c == 0, z, y)
+    own_last = jnp.where(c == 0, z, (y + 2) % 4)
 
     def last_head(z_, c_):
         return c_ * HALF + 16 + z_
@@ -291,7 +299,7 @@
                 if c_ == 0:
                     w_, to, other = (z + d) % 4, dev((z + d) % 4, y, xh, 0), c
                 else:
-                    w_, to, other = (y + d) % 4, dev(z, (y + d) % 4, xh, 1), 1 - c
+                    w_, to, other = (y + d + 2) % 4, dev(z, (y + d) % 4, xh, 1), 1 - c
                 slot = jnp.maximum(2 * d + other, 1) - 1
                 cols = columns(last_head(w_, c_))
                 for n, x in ((1, x2), (0, x1)):
@@ -315,6 +323,10 @@
             cr = dot_t(left, x2o[4, j])
             total = cr if total is None else total + cr
         r["d4"][...] = r["d4"][...] + total if which else total
+
+    def exchange_sent(i):
+        part = x2o.at[i // 2, pl.ds(4 * (i % 2), 4)]
+        rcopy(part, part, r["x_s"].at[i], r["x_q"].at[i], twin).wait_send()
 
     load1 = pltpu.make_async_copy(r["x1_hbm"].at[0], x1, r["l_s"].at[0])
     load2 = pltpu.make_async_copy(r["x2_hbm"].at[0], x2, r["l_s"].at[1])
@@ -400,12 +412,12 @@
             r[name + "x_acc"][p] = (buf[p, c, u] + r2[p, 0]) + (r2[p, 1] + r2[p, 2])
 
     def last_s3():
-        away = jnp.where(c == 0, y - z + 4, z - y + 4) % 4
+        away = jnp.where(c == 0, y - z + 4, z - own_last + 4) % 4
         slot = away * 2 + 1 - xh
         launch(
             rcopy(
                 r["d4"], r["r5"].at[slot], r["d4_s"].at[0], r["d4_q"].at[slot],
-                dev(own_last, own_last, 1, c),
+                dev(own_last, (own_last + 2 * c) % 4, 1, c),
             ),
             no(late_owner),
         )
@@ -428,7 +440,7 @@
     def similarity(raw, means, w2):
         white = mm(mm(r["w12"][0], raw / tokens - means), w2)
         sq = jnp.sum(jnp.sum(white * white, axis=1, keepdims=True), axis=0, keepdims=True)
-        return jnp.broadcast_to(sq / HD, (8, HD))
+        return jnp.broadcast_to(sq / HD, (1, HD))
 
     def whiten():
         top = s4_total("pa", True)
@@ -517,25 +529,31 @@
     cross_s2_sum(1)
 
     lane_head = c * HALF + jnp.where(own == 4, 16 + z, head_of(z, own))
-    here = iota((8, HD), 1) == lane_head
+    lanes = iota((1, HD), 1)
     sa_mine = r["sa"].at[(c * 4 + z) * 5 + own]
 
     def own_similarity():
         raw = jnp.concatenate([s4_total("ca", True), s4_total("cb", True)], axis=0)
         sim = similarity(raw, mean_term(r["aux"][1:2, :]), r["w12"][1])
-        sa_mine[...] = jnp.where(jnp.logical_and(here, row8 == lay), sim, 0.0)
+        sa_mine[...] = jnp.where(lanes == 64 * lay + lane_head, sim, 0.0)
         arrive(r["w_in_x"], r["y_q"].at[0])
         r["means"][...] = mean_term(r["w_in_x"][HD + 1 : HD + 2])
 
     def other_similarity(raw):
         sim = similarity(raw, r["means"][...], r["w_in_x"][0:HD])
-        sa_mine[...] = jnp.where(jnp.logical_and(here, row8 == 1 - lay), sim, sa_mine[...])
-
-        def send(i):
-            to = (tok + 1 + (25 + i) % others) % (others + 1)
-            rcopy(sa_mine, sa_mine, r["sa_s"].at[0], r["sa_q"].at[0], (to, lay)).start()
-
-        loop(others, send, unroll=9)
+        sa_mine[...] = jnp.where(lanes == 64 * (1 - lay) + lane_head, sim, sa_mine[...])
+        steps = (2, 1, 3, 0)
+        z_at = [(z + d) % 4 * 16 for d in range(4)]
+        y_at = [(y + d) % 4 * 4 for d in range(4)]
+        x_at = [(xh + d) % 2 * 2 for d in range(2)]
+        c_at = [(c + d) % 2 for d in range(2)]
+        for dx in (1, 0):
+            for dz in steps:
+                for dy in steps:
+                    for dc in (1, 0):
+                        if dx or dz or dy or dc:
+                            to = z_at[dz] + y_at[dy] + (x_at[dx] + c_at[dc])
+                            rcopy(sa_mine, sa_mine, r["sa_s"].at[0], r["sa_q"].at[0], (to, lay)).start()
 
     def emit(h):
         ch, zz, yy, p = places(h)
@@ -553,6 +571,9 @@
         s3(name + "x", axis, range(3))
     for name in ("ca", "cb"):
         s3_sum(name, True)
+    early = list(pending)
+    pending.clear()
+    for name in ("ca", "cb"):
         s4(name, True)
     for name in GATHERS:
         g4_arrive(name)
@@ -561,6 +582,9 @@
     for name, axis in LATE.items():
         s3(name + "x", axis, (3,))
     collected(0)
+    drain(early)
+    for i in range(2 * PARTS - 2):
+        exchange_sent(i)
     last_cross(0)
     last_cross(1)
     last_s3()
@@ -582,16 +606,12 @@
     total = r["sa"][0]
     for i in range(1, HEADS):
         total = total + r["sa"][i]
-    r["sim"][...] = total[0:2, 0:HEADS]
-
-    for cond, copy in pending:
-        if cond is None:
-            copy.wait_send()
-        else:
-            pl.when(cond)(lambda copy=copy: copy.wait_send())
-    for i in range(2 * PARTS):
-        part = x2o.at[i // 2, pl.ds(4 * (i % 2), 4)]
-        rcopy(part, part, r["x_s"].at[i], r["x_q"].at[i], twin).wait_send()
+    r["sim"][0:1, :] = total[:, 0:HEADS]
+    r["sim"][1:2, :] = total[:, 64 : 64 + HEADS]
+
+    drain(pending)
+    for i in (2 * PARTS - 2, 2 * PARTS - 1):
+        exchange_sent(i)
 
     @pl.when(owner)
     def _():
@@ -643,7 +663,7 @@
         add(name + "_r4", pltpu.VMEM((n, HD), F32))
         add(name + "_s", dma(10))
         add(name + "_q", dma(11))
-    add("sa", pltpu.VMEM((64, 8, HD), F32))
+    add("sa", pltpu.VMEM((64, 1, HD), F32))
     for name, (n, _) in GATHERS.items():
         add(name, pltpu.VMEM((2, 4, 5, n, HD), F32))
         add(name + "_s", dma(11))

time: 88.7 us -> 87 us (0.981)
  Pallas kernels: 88 us -> 86.3 us
    pallas_call x1, Pallas kernels: 85.6 us -> 83.9 us  [gather_kernel(): pl.pallas_call(functools.partial(kernel, tokens, names), out_shape=(pltpu...]
where the time goes in v6:
time: 87 us; the launch traced here: 86.9 us
  Pallas kernels  86.3 us (99%)
    pallas_call x1, Pallas kernels, gather_kernel(): pl.pallas_call(functools.partial(kernel, tokens, names), out_shape=(pltpu...  83.9 us
    pallas_call x1, Pallas kernels, store(): pl.pallas_call(store_kernel, out_shape=(jax.ShapeDtypeStruct((2, 1, HEADS...  2.43 us

profile of v6, /device:TPU:1, one launch (start us, length us, event | category | flops | bytes accessed | tf_op | source)
XLA Modules:
  0.0 86.9 jit_solution(3643523574482644007)
XLA Ops:
  0.6 83.9 %shard_map.41 = (f32[2,40,128,128]{3,2,1,0:T(8,128)S(1)}, f32[2,40]{1,0:T(2,128)S(1)}) custom-call(bf16[1,256,5120]{2,1,0:T(8,128)(2,1)} %refs_0_.1, bf16[1,256,5120]{2,1,0:T(8,128)(2,1)} %refs_1_.1), custom_call_target="tpu_custom_call" | custom-call | tf_op jit(solution)/shard_map/pallas_call | solution.py:683
  84.5 2.4 %shard_map.42 = (f32[2,1,40,128,128]{4,3,2,1,0:T(8,128)}, f32[1,2,40]{2,1,0:T(2,128)}) custom-call(f32[2,40,128,128]{3,2,1,0:T(8,128)S(1)} %get-tuple-element.4.w, f32[2,40]{1,0:T(2,128)S(1)} %get-tuple-element.5.sim), custom_call_target="tpu_custom_call" | custom-call | tf_op jit(solution)/shard_map/pallas_call | solution.py:722

commit v7 on v6

--- a/solution.py
+++ b/solution.py
@@ -15,6 +15,7 @@
 PARTS = 5
 FROM_HBM = 3
 BATCHES = (14, 21, 32)
+CARRIED = (3, 7)
 VMEM_LIMIT = 48 * 2**20
 F32 = jnp.float32
 HI = lax.Precision.HIGHEST
@@ -51,6 +52,21 @@
     first = jnp.where(upper, p, pt)
     second = jnp.where(upper, jnp.where(diag, aux[2:3, :], pt), p)
     return first, second
+
+
+def fold(w):
+    row, lane = iota((64, HD), 0), iota((64, HD), 1)
+    lower = jnp.logical_and(lane < 64, row > lane)
+    return jnp.where(lower, pltpu.roll(w[64:], 64, 1), w[:64])
+
+
+def unfold(folded, diagonal):
+    row, lane = iota((HD, HD), 0), iota((HD, HD), 1)
+    q = jnp.concatenate([folded, pltpu.roll(folded, 64, 1)], axis=0)
+    top = jnp.logical_and(row < 64, row <= lane)
+    low = jnp.logical_and(lane >= 64, row > lane)
+    out = jnp.where(jnp.logical_or(top, low), q, q.T)
+    return jnp.where(jnp.logical_and(row == lane, row >= 64), diagonal, out)
 
 
 def head_of(z, p):
@@ -291,7 +307,20 @@
             if p == 4:
                 src = x2.at[:, columns(last_head(own_last, c))] if j == 0 else r["m2"].at[j - 1]
             sem = 2 * p + j // 4
-            rcopy(src, x2o.at[p, j], r["x_s"].at[sem], r["x_q"].at[sem], twin).start()
+            copy = rcopy(src, x2o.at[p, j], r["x_s"].at[sem], r["x_q"].at[sem], twin)
+            if p == 4 and j in CARRIED:
+                pl.when(c == 1)(lambda copy=copy: copy.start())
+            else:
+                copy.start()
+            if n == 8 * PARTS - 5:
+                for i, k in enumerate(CARRIED):
+                    launch(
+                        rcopy(
+                            r["m3"].at[i], x2o.at[4, k], r["m3_s"].at[2 + i], r["x_q"].at[8 + k // 4],
+                            (jnp.maximum(tok, 1) - 1, 1 - lay),
+                        ),
+                        c == 1,
+                    )
 
     def collect():
         for d in (1, 3, 2, 0):
@@ -303,17 +332,33 @@
                 slot = jnp.maximum(2 * d + other, 1) - 1
                 cols = columns(last_head(w_, c_))
                 for n, x in ((1, x2), (0, x1)):
+                    cond = None if d else other == 1
+                    carried = n == 1 and c_ == 0 and 2 * d + 1 in CARRIED
+                    if carried:
+                        i = CARRIED.index(2 * d + 1)
+                        launch(
+                            rcopy(
+                                x.at[:, cols], r["m3"].at[i], r["m3_s"].at[i], r["m3_q"].at[i],
+                                dev(w_, y, xh, 1),
+                            ),
+                            c == 1,
+                        )
+                        cond = c == 0
                     launch(
                         rcopy(
                             x.at[:, cols], r["m%d" % (n + 1)].at[slot], r["m_s"].at[8 * n + 2 * d + c_],
                             r["m_q"].at[7 * n + slot], to,
                         ),
-                        None if d else other == 1,
+                        cond,
                     )
 
     def collected(n):
         for j in range(1, 8):
-            arrive(r["m%d" % (n + 1)].at[j - 1], r["m_q"].at[7 * n + j - 1])
+            carried = n == 1 and j in CARRIED
+            arrive(r["m%d" % (n + 1)].at[j - 1], r["m_q"].at[7 * n + j - 1], c == 1 if carried else None)
+        if n == 1:
+            for i in range(2):
+                arrive(r["m3"].at[i], r["m3_q"].at[i], c == 1)
 
     def last_cross(which):
         arrive(x2o.at[4, pl.ds(4 * which, 4)], r["x_q"].at[8 + which])
@@ -325,8 +370,15 @@
         r["d4"][...] = r["d4"][...] + total if which else total
 
     def exchange_sent(i):
-        part = x2o.at[i // 2, pl.ds(4 * (i % 2), 4)]
-        rcopy(part, part, r["x_s"].at[i], r["x_q"].at[i], twin).wait_send()
+        def sent(count):
+            part = x2o.at[i // 2, pl.ds(4 * (i % 2), count)]
+            rcopy(part, part, r["x_s"].at[i], r["x_q"].at[i], twin).wait_send()
+
+        if i < 8:
+            sent(4)
+        else:
+            pl.when(c == 1)(lambda: sent(4))
+            pl.when(c == 0)(lambda: sent(3))
 
     load1 = pltpu.make_async_copy(r["x1_hbm"].at[0], x1, r["l_s"].at[0])
     load2 = pltpu.make_async_copy(r["x2_hbm"].at[0], x2, r["l_s"].at[1])
@@ -477,8 +529,8 @@
         r["w12"][0] = w1
         r["w12"][1] = w2
         r["aux"][...] = aux
-        r["w_out_x"][0:HD] = w2
-        r["w_out_x"][HD : HD + 8] = aux
+        r["w_out_x"][0:64] = fold(w2)
+        r["w_out_x"][64:72] = jnp.where(row8 == 2, jnp.broadcast_to(wd, (8, HD)), aux)
     def both(p):
         cross(p, 0)
         cross(p, 1)
@@ -537,10 +589,11 @@
         sim = similarity(raw, mean_term(r["aux"][1:2, :]), r["w12"][1])
         sa_mine[...] = jnp.where(lanes == 64 * lay + lane_head, sim, 0.0)
         arrive(r["w_in_x"], r["y_q"].at[0])
-        r["means"][...] = mean_term(r["w_in_x"][HD + 1 : HD + 2])
+        r["means"][...] = mean_term(r["w_in_x"][65:66])
+        r["w2_other"][...] = unfold(r["w_in_x"][0:64], r["w_in_x"][66:67])
 
     def other_similarity(raw):
-        sim = similarity(raw, r["means"][...], r["w_in_x"][0:HD])
+        sim = similarity(raw, r["means"][...], r["w2_other"][...])
         sa_mine[...] = jnp.where(lanes == 64 * (1 - lay) + lane_head, sim, sa_mine[...])
         steps = (2, 1, 3, 0)
         z_at = [(z + d) % 4 * 16 for d in range(4)]
@@ -575,12 +628,12 @@
     pending.clear()
     for name in ("ca", "cb"):
         s4(name, True)
+    cross_s2_sum(3)
+    for name, axis in LATE.items():
+        s3(name + "x", axis, (3,))
     for name in GATHERS:
         g4_arrive(name)
     loop(HEADS, emit, unroll=2)
-    cross_s2_sum(3)
-    for name, axis in LATE.items():
-        s3(name + "x", axis, (3,))
     collected(0)
     drain(early)
     for i in range(2 * PARTS - 2):
@@ -649,6 +702,9 @@
         add(name + "_q", dma(17))
     for name in ("m1", "m2"):
         add(name, pltpu.VMEM((7, rows, HD), first_acts.dtype))
+    add("m3", pltpu.VMEM((2, rows, HD), first_acts.dtype))
+    add("m3_s", dma(4))
+    add("m3_q", dma(2))
     add("m_s", dma(16))
     add("m_q", dma(14))
     add("d4", pltpu.VMEM((HD, HD), F32))
@@ -672,8 +728,9 @@
     add("sa_q", dma(1))
     add("w12", pltpu.VMEM((2, HD, HD), F32))
     add("aux", pltpu.VMEM((8, HD), F32))
-    add("w_out_x", pltpu.VMEM((HD + 8, HD), F32))
-    add("w_in_x", pltpu.VMEM((HD + 8, HD), F32))
+    add("w_out_x", pltpu.VMEM((72, HD), F32))
+    add("w_in_x", pltpu.VMEM((72, HD), F32))
+    add("w2_other", pltpu.VMEM((HD, HD), F32))
     add("l_s", dma(2))
     add("x_s", dma(2 * PARTS))
     add("x_q", dma(2 * PARTS))

time: 87 us -> 85.9 us (0.987)
  Pallas kernels: 86.3 us -> 85.2 us
    pallas_call x1, Pallas kernels: 83.9 us -> 82.8 us  [gather_kernel(): pl.pallas_call(functools.partial(kernel, tokens, names), out_shape=(pltpu...]
where the time goes in v7:
time: 85.9 us; the launch traced here: 85.8 us
  Pallas kernels  85.2 us (99%)
    pallas_call x1, Pallas kernels, gather_kernel(): pl.pallas_call(functools.partial(kernel, tokens, names), out_shape=(pltpu...  82.8 us
    pallas_call x1, Pallas kernels, store(): pl.pallas_call(store_kernel, out_shape=(jax.ShapeDtypeStruct((2, 1, HEADS...  2.43 us

profile of v7, /device:TPU:1, one launch (start us, length us, event | category | flops | bytes accessed | tf_op | source)
XLA Modules:
  0.0 85.8 jit_solution(5137609684166063949)
XLA Ops:
  0.6 82.8 %shard_map.41 = (f32[2,40,128,128]{3,2,1,0:T(8,128)S(1)}, f32[2,40]{1,0:T(2,128)S(1)}) custom-call(bf16[1,256,5120]{2,1,0:T(8,128)(2,1)} %refs_0_.1, bf16[1,256,5120]{2,1,0:T(8,128)(2,1)} %refs_1_.1), custom_call_target="tpu_custom_call" | custom-call | tf_op jit(solution)/shard_map/pallas_call | solution.py:740
  83.4 2.4 %shard_map.42 = (f32[2,1,40,128,128]{4,3,2,1,0:T(8,128)}, f32[1,2,40]{2,1,0:T(2,128)}) custom-call(f32[2,40,128,128]{3,2,1,0:T(8,128)S(1)} %get-tuple-element.4.w, f32[2,40]{1,0:T(2,128)S(1)} %get-tuple-element.5.sim), custom_call_target="tpu_custom_call" | custom-call | tf_op jit(solution)/shard_map/pallas_call | solution.py:779

commit v8 on v7

--- a/solution.py
+++ b/solution.py
@@ -14,7 +14,7 @@
 HALF = HEADS // 2
 PARTS = 5
 FROM_HBM = 3
-BATCHES = (14, 21, 32)
+BATCHES = (15, 21, 32)
 CARRIED = (3, 7)
 VMEM_LIMIT = 48 * 2**20
 F32 = jnp.float32
@@ -132,24 +132,21 @@
         )
 
     others = lax.axis_size("tok") - 1
-    pending = []
-
     def launch(copy, cond=None):
-        pending.append((cond, copy))
         if cond is None:
             copy.start()
         else:
             pl.when(cond)(lambda: copy.start())
 
-    def drain(copies):
-        for cond, copy in copies:
-            if cond is None:
-                copy.wait_send()
-            else:
-                pl.when(cond)(lambda copy=copy: copy.wait_send())
+    def left(ref, sem, cond=None):
+        copy = rcopy(ref, ref, sem, r["l_s"].at[0], twin)
+        if cond is None:
+            copy.wait_send()
+        else:
+            pl.when(cond)(lambda: copy.wait_send())
 
     def arrive(ref, sem, cond=None):
-        copy = rcopy(ref, ref, r["none"].at[0], sem, twin)
+        copy = rcopy(ref, ref, r["l_s"].at[0], sem, twin)
         if cond is None:
             copy.wait_recv()
         else:
@@ -182,16 +179,15 @@
             to = (u + d) % 4
             launch(
                 rcopy(
-                    r[name].at[c, to], r[name + "_r2"].at[d - 1], r[name + "_s"].at[d],
-                    r[name + "_q"].at[d], dev_uv(axis, to, v, xh),
+                    r[name].at[c, to], r[name + "_r2"].at[d - 1], r[name + "_s"].at[1],
+                    r[name + "_q"].at[1], dev_uv(axis, to, v, xh),
                 )
             )
 
     def s2_sum(name):
         u, _ = uv(CHAINS[name][1])
         buf, r2, acc = r[name], r[name + "_r2"], r[name + "_acc"]
-        for d in (1, 2, 3):
-            arrive(r2.at[d - 1], r[name + "_q"].at[d])
+        arrive(r2, r[name + "_q"].at[1])
         for s in range(5):
             acc[s] = (buf[c, u, s] + r2[0, s]) + (r2[1, s] + r2[2, s])
 
@@ -203,8 +199,8 @@
             kind = p // 4
             launch(
                 rcopy(
-                    r[name + "_acc"].at[p], r[name + "_r3"].at[kind, off], r[name + "_s"].at[4 + p],
-                    r[name + "_q"].at[4 + kind * 3 + off], dev_uv(axis, u, vo, xh),
+                    r[name + "_acc"].at[p], r[name + "_r3"].at[kind, off], r[name + "_s"].at[2],
+                    r[name + "_q"].at[2 + kind], dev_uv(axis, u, vo, xh),
                 ),
                 v != vo,
             )
@@ -213,8 +209,7 @@
         acc, r3, part = r[name + "_acc"], r[name + "_r3"], r[name + "_t"]
 
         def add(kind, slot):
-            for off in range(3):
-                arrive(r3.at[kind, off], r[name + "_q"].at[4 + kind * 3 + off])
+            arrive(r3.at[kind], r[name + "_q"].at[2 + kind])
             part[kind] = (acc[slot] + r3[kind, 0]) + (r3[kind, 1] + r3[kind, 2])
 
         add(0, main)
@@ -224,12 +219,22 @@
     def s4(name, extra):
         src = r[name + "_t"].at[extra_give] if extra else r[name + "_t"].at[0]
         cond = gives if extra else no(owns_main)
-        launch(rcopy(src, r[name + "_r4"], r[name + "_s"].at[9], r[name + "_q"].at[10], far), cond)
+        launch(rcopy(src, r[name + "_r4"], r[name + "_s"].at[3], r[name + "_q"].at[4], far), cond)
 
     def s4_total(name, extra):
-        arrive(r[name + "_r4"], r[name + "_q"].at[10])
+        arrive(r[name + "_r4"], r[name + "_q"].at[4])
         mine = r[name + "_t"][extra_mine] if extra else r[name + "_t"][0]
         return mine + r[name + "_r4"][...]
+
+    def chain_left(name):
+        acc = r[name + "_acc"]
+        left(r[name + "_r1"], r[name + "_s"].at[0])
+        left(r[name + "_r2"], r[name + "_s"].at[1])
+        left(acc.at[pl.ds(0, 3)], r[name + "_s"].at[2], on_diag)
+        left(acc.at[pl.ds(0, 4)], r[name + "_s"].at[2], no(on_diag))
+
+    def given(name, cond):
+        left(r[name + "_r4"], r[name + "_s"].at[3], cond)
 
     def g1(name):
         u, _ = uv(GATHERS[name][1])
@@ -249,17 +254,16 @@
                 place = r[name].at[c, u, slot]
                 launch(
                     rcopy(
-                        place, place, r[name + "_s"].at[kind * 3 + d], r[name + "_q"].at[1 + slot],
+                        place, place, r[name + "_s"].at[1], r[name + "_q"].at[1],
                         dev_uv(axis, u, (v + d) % 4, xh),
                     ),
                     on_diag if kind else None,
                 )
 
     def g2_arrive(name):
-        axis = GATHERS[name][1]
-        u, v = uv(axis)
-        for p in range(5):
-            arrive(r[name].at[c, u, p], r[name + "_q"].at[1 + p], v != target(axis, p))
+        u, _ = uv(GATHERS[name][1])
+        arrive(r[name].at[c, u, pl.ds(0, 3)], r[name + "_q"].at[1], on_diag)
+        arrive(r[name].at[c, u, pl.ds(0, 4)], r[name + "_q"].at[1], no(on_diag))
 
     def g3(name):
         axis = GATHERS[name][1]
@@ -268,22 +272,28 @@
         for d in (1, 3, 2):
             launch(
                 rcopy(
-                    place, place, r[name + "_s"].at[6 + d], r[name + "_q"].at[5 + d],
+                    place, place, r[name + "_s"].at[2], r[name + "_q"].at[2],
                     dev_uv(axis, (u + d) % 4, v, xh),
                 )
             )
 
     def g3_arrive(name):
-        u, _ = uv(GATHERS[name][1])
-        for d in (1, 2, 3):
-            arrive(r[name].at[c, (u - d + 4) % 4], r[name + "_q"].at[5 + d])
+        arrive(r[name].at[c, pl.ds(0, 3)], r[name + "_q"].at[2])
 
     def g4(name):
         place = r[name].at[c]
-        launch(rcopy(place, place, r[name + "_s"].at[10], r[name + "_q"].at[9], sibling))
+        launch(rcopy(place, place, r[name + "_s"].at[3], r[name + "_q"].at[3], sibling))
 
     def g4_arrive(name):
-        arrive(r[name].at[1 - c], r[name + "_q"].at[9])
+        arrive(r[name].at[1 - c], r[name + "_q"].at[3])
+
+    def gather_left(name):
+        buf, sems = r[name], r[name + "_s"]
+        left(buf.at[c, 0, 0], sems.at[0], owner)
+        left(buf.at[c, pl.ds(0, 2), pl.ds(0, 3)], sems.at[1], on_diag)
+        left(buf.at[c, 0, pl.ds(0, 3)], sems.at[1], no(on_diag))
+        left(buf.at[c, pl.ds(0, 3)], sems.at[2])
+        left(buf.at[c], sems.at[3])
 
     x1, x2, x2o = r["x1"], r["x2"], r["x2o"]
 
@@ -307,7 +317,7 @@
             if p == 4:
                 src = x2.at[:, columns(last_head(own_last, c))] if j == 0 else r["m2"].at[j - 1]
             sem = 2 * p + j // 4
-            copy = rcopy(src, x2o.at[p, j], r["x_s"].at[sem], r["x_q"].at[sem], twin)
+            copy = rcopy(src, x2o.at[p, j], r["x_s"].at[p // 4], r["x_q"].at[sem], twin)
             if p == 4 and j in CARRIED:
                 pl.when(c == 1)(lambda copy=copy: copy.start())
             else:
@@ -316,7 +326,7 @@
                 for i, k in enumerate(CARRIED):
                     launch(
                         rcopy(
-                            r["m3"].at[i], x2o.at[4, k], r["m3_s"].at[2 + i], r["x_q"].at[8 + k // 4],
+                            r["m3"].at[i], x2o.at[4, k], r["x_s"].at[1], r["x_q"].at[8 + k // 4],
                             (jnp.maximum(tok, 1) - 1, 1 - lay),
                         ),
                         c == 1,
@@ -338,7 +348,7 @@
                         i = CARRIED.index(2 * d + 1)
                         launch(
                             rcopy(
-                                x.at[:, cols], r["m3"].at[i], r["m3_s"].at[i], r["m3_q"].at[i],
+                                x.at[:, cols], r["m3"].at[i], r["m_s"].at[1], r["m_q"].at[2],
                                 dev(w_, y, xh, 1),
                             ),
                             c == 1,
@@ -346,19 +356,19 @@
                         cond = c == 0
                     launch(
                         rcopy(
-                            x.at[:, cols], r["m%d" % (n + 1)].at[slot], r["m_s"].at[8 * n + 2 * d + c_],
-                            r["m_q"].at[7 * n + slot], to,
+                            x.at[:, cols], r["m%d" % (n + 1)].at[slot], r["m_s"].at[n],
+                            r["m_q"].at[n], to,
                         ),
                         cond,
                     )
 
     def collected(n):
-        for j in range(1, 8):
-            carried = n == 1 and j in CARRIED
-            arrive(r["m%d" % (n + 1)].at[j - 1], r["m_q"].at[7 * n + j - 1], c == 1 if carried else None)
-        if n == 1:
-            for i in range(2):
-                arrive(r["m3"].at[i], r["m3_q"].at[i], c == 1)
+        if n == 0:
+            arrive(r["m1"], r["m_q"].at[0])
+        else:
+            arrive(r["m2"], r["m_q"].at[1], c == 1)
+            arrive(r["m2"].at[pl.ds(0, 7 - len(CARRIED))], r["m_q"].at[1], c == 0)
+            arrive(r["m3"], r["m_q"].at[2], c == 1)
 
     def last_cross(which):
         arrive(x2o.at[4, pl.ds(4 * which, 4)], r["x_q"].at[8 + which])
@@ -369,16 +379,12 @@
             total = cr if total is None else total + cr
         r["d4"][...] = r["d4"][...] + total if which else total
 
-    def exchange_sent(i):
-        def sent(count):
-            part = x2o.at[i // 2, pl.ds(4 * (i % 2), count)]
-            rcopy(part, part, r["x_s"].at[i], r["x_q"].at[i], twin).wait_send()
-
-        if i < 8:
-            sent(4)
+    def exchange_left(last):
+        if last:
+            left(x2o.at[pl.ds(0, 2), pl.ds(0, 5)], r["x_s"].at[1], c == 1)
+            left(x2o.at[0, pl.ds(0, 6)], r["x_s"].at[1], c == 0)
         else:
-            pl.when(c == 1)(lambda: sent(4))
-            pl.when(c == 0)(lambda: sent(3))
+            left(x2o.at[pl.ds(0, 4)], r["x_s"].at[0])
 
     load1 = pltpu.make_async_copy(r["x1_hbm"].at[0], x1, r["l_s"].at[0])
     load2 = pltpu.make_async_copy(r["x2_hbm"].at[0], x2, r["l_s"].at[1])
@@ -434,51 +440,49 @@
                 for name in LATE:
                     launch(
                         rcopy(
-                            r[name].at[p, 1 - c], r[name + "_r1"].at[p], r[name + "_s"].at[p],
-                            r[name + "_q"].at[p], sibling,
+                            r[name].at[p, 1 - c], r[name + "_r1"].at[p], r["late_s"].at[0],
+                            r["late_q"].at[p], sibling,
                         )
                     )
 
     def cross_s2(p):
+        arrive(r["da_r1"].at[pl.ds(0, 2)], r["late_q"].at[p])
         for name, axis in LATE.items():
             buf, r1 = r[name], r[name + "_r1"]
             u, v = uv(axis)
-            arrive(r1.at[p], r[name + "_q"].at[p])
             for i in range(4):
                 buf[p, c, i] = buf[p, c, i] + r1[p, i]
             for d in (1, 3, 2):
                 to = (u + d) % 4
                 launch(
                     rcopy(
-                        buf.at[p, c, to], r[name + "_r2"].at[p, d - 1], r[name + "_s"].at[2 + 3 * (p + 1) + d - 1],
-                        r[name + "_q"].at[2 + 3 * (p + 1) + d - 1], dev_uv(axis, to, v, xh),
+                        buf.at[p, c, to], r[name + "_r2"].at[p, d - 1], r["late_s"].at[1],
+                        r["late_q"].at[4 + p], dev_uv(axis, to, v, xh),
                     )
                 )
 
     def cross_s2_sum(p):
+        arrive(r["da_r2"].at[pl.ds(0, 2)], r["late_q"].at[4 + p])
         for name, axis in LATE.items():
             buf, r2 = r[name], r[name + "_r2"]
             u, _ = uv(axis)
-            for d in (1, 2, 3):
-                arrive(r2.at[p, d - 1], r[name + "_q"].at[2 + 3 * (p + 1) + d - 1])
             r[name + "x_acc"][p] = (buf[p, c, u] + r2[p, 0]) + (r2[p, 1] + r2[p, 2])
 
     def last_s3():
         away = jnp.where(c == 0, y - z + 4, z - own_last + 4) % 4
-        slot = away * 2 + 1 - xh
+        slot = jnp.maximum(away * 2 + 1 - xh, 1)
         launch(
             rcopy(
-                r["d4"], r["r5"].at[slot], r["d4_s"].at[0], r["d4_q"].at[slot],
+                r["d4"], r["r5"].at[slot - 1], r["d4_s"].at[0], r["d4_q"].at[0],
                 dev(own_last, (own_last + 2 * c) % 4, 1, c),
             ),
             no(late_owner),
         )
 
     def last_total():
-        for slot in range(1, 8):
-            arrive(r["r5"].at[slot], r["d4_q"].at[slot])
-        total = r["d4"][...] + r["r5"][1]
-        for slot in range(2, 8):
+        arrive(r["r5"], r["d4_q"].at[0])
+        total = r["d4"][...] + r["r5"][0]
+        for slot in range(1, 7):
             total = total + r["r5"][slot]
         return total
 
@@ -624,8 +628,6 @@
         s3(name + "x", axis, range(3))
     for name in ("ca", "cb"):
         s3_sum(name, True)
-    early = list(pending)
-    pending.clear()
     for name in ("ca", "cb"):
         s4(name, True)
     cross_s2_sum(3)
@@ -635,9 +637,17 @@
         g4_arrive(name)
     loop(HEADS, emit, unroll=2)
     collected(0)
-    drain(early)
-    for i in range(2 * PARTS - 2):
-        exchange_sent(i)
+    for name in CHAINS:
+        chain_left(name)
+    for name in ("pa", "pb"):
+        given(name, gives)
+    for name in GATHERS:
+        gather_left(name)
+    for n in (0, 1):
+        left(r["m1"], r["m_s"].at[n])
+    left(r["da"], r["late_s"].at[0])
+    left(r["da"].at[pl.ds(0, 3)], r["late_s"].at[1])
+    exchange_left(False)
     last_cross(0)
     last_cross(1)
     last_s3()
@@ -662,19 +672,15 @@
     r["sim"][0:1, :] = total[:, 0:HEADS]
     r["sim"][1:2, :] = total[:, 64 : 64 + HEADS]
 
-    drain(pending)
-    for i in (2 * PARTS - 2, 2 * PARTS - 1):
-        exchange_sent(i)
-
-    @pl.when(owner)
-    def _():
-        for name in GATHERS:
-            u, _ = uv(GATHERS[name][1])
-            place = r[name].at[c, u, own]
-            rcopy(place, place, r[name + "_s"].at[0], r[name + "_q"].at[0], far).wait_send()
-        rcopy(r["w_out_x"], r["w_in_x"], r["y_s"].at[0], r["y_q"].at[0], twin).wait_send()
-        sent = r["sa"].at[pl.ds(0, others)]
-        rcopy(sent, sent, r["sa_s"].at[0], r["sa_q"].at[0], far).wait_send()
+    exchange_left(True)
+    for name in ("ca", "cb"):
+        given(name, gives)
+    for name in LATE:
+        left(r[name + "x_acc"].at[pl.ds(0, 3)], r[name + "x_s"].at[2])
+        given(name + "x", no(owns_main))
+    left(r["d4"], r["d4_s"].at[0], no(late_owner))
+    left(r["w_out_x"], r["y_s"].at[0], owner)
+    left(r["sa"].at[pl.ds(0, others)], r["sa_s"].at[0], owner)
 
 
 def gather_kernel(tokens, first_acts, second_acts):
@@ -698,32 +704,30 @@
         add(name, pltpu.VMEM((PARTS - 1, 2, 4, 64, HD), F32))
         add(name + "_r1", pltpu.VMEM((PARTS - 1, 4, 64, HD), F32))
         add(name + "_r2", pltpu.VMEM((PARTS - 1, 3, 64, HD), F32))
-        add(name + "_s", dma(17))
-        add(name + "_q", dma(17))
+    add("late_s", dma(2))
+    add("late_q", dma(8))
     for name in ("m1", "m2"):
         add(name, pltpu.VMEM((7, rows, HD), first_acts.dtype))
     add("m3", pltpu.VMEM((2, rows, HD), first_acts.dtype))
-    add("m3_s", dma(4))
-    add("m3_q", dma(2))
-    add("m_s", dma(16))
-    add("m_q", dma(14))
+    add("m_s", dma(2))
+    add("m_q", dma(3))
     add("d4", pltpu.VMEM((HD, HD), F32))
-    add("r5", pltpu.VMEM((8, HD, HD), F32))
+    add("r5", pltpu.VMEM((7, HD, HD), F32))
     add("d4_s", dma(1))
-    add("d4_q", dma(8))
+    add("d4_q", dma(1))
     add("means", pltpu.VMEM((HD, HD), F32))
     for name, n in [(k, v[0]) for k, v in CHAINS.items()] + [(k + "x", 64) for k in LATE]:
         add(name + "_acc", pltpu.VMEM((5, n, HD), F32))
         add(name + "_r3", pltpu.VMEM((2, 3, n, HD), F32))
         add(name + "_t", pltpu.VMEM((2, n, HD), F32))
         add(name + "_r4", pltpu.VMEM((n, HD), F32))
-        add(name + "_s", dma(10))
-        add(name + "_q", dma(11))
+        add(name + "_s", dma(4))
+        add(name + "_q", dma(5))
     add("sa", pltpu.VMEM((64, 1, HD), F32))
     for name, (n, _) in GATHERS.items():
         add(name, pltpu.VMEM((2, 4, 5, n, HD), F32))
-        add(name + "_s", dma(11))
-        add(name + "_q", dma(10))
+        add(name + "_s", dma(4))
+        add(name + "_q", dma(4))
     add("sa_s", dma(1))
     add("sa_q", dma(1))
     add("w12", pltpu.VMEM((2, HD, HD), F32))
@@ -732,11 +736,10 @@
     add("w_in_x", pltpu.VMEM((72, HD), F32))
     add("w2_other", pltpu.VMEM((HD, HD), F32))
     add("l_s", dma(2))
-    add("x_s", dma(2 * PARTS))
+    add("x_s", dma(2))
     add("x_q", dma(2 * PARTS))
     add("y_s", dma(1))
     add("y_q", dma(1))
-    add("none", dma(1))
     return pl.pallas_call(
         functools.partial(kernel, tokens, names),
         out_shape=(

time: 85.9 us -> 83.1 us (0.967)
  Pallas kernels: 85.2 us -> 82.4 us
    pallas_call x1, Pallas kernels: 82.8 us -> 80 us  [gather_kernel(): pl.pallas_call(functools.partial(kernel, tokens, names), out_shape=(pltpu...]
where the time goes in v8:
time: 83.1 us; the launch traced here: 83 us
  Pallas kernels  82.4 us (99%)
    pallas_call x1, Pallas kernels, gather_kernel(): pl.pallas_call(functools.partial(kernel, tokens, names), out_shape=(pltpu...  80 us
    pallas_call x1, Pallas kernels, store(): pl.pallas_call(store_kernel, out_shape=(jax.ShapeDtypeStruct((2, 1, HEADS...  2.43 us

profile of v8, /device:TPU:1, one launch (start us, length us, event | category | flops | bytes accessed | tf_op | source)
XLA Modules:
  0.0 83.0 jit_solution(2752784437489591670)
XLA Ops:
  0.6 80.0 %shard_map.41 = (f32[2,40,128,128]{3,2,1,0:T(8,128)S(1)}, f32[2,40]{1,0:T(2,128)S(1)}) custom-call(bf16[1,256,5120]{2,1,0:T(8,128)(2,1)} %refs_0_.1, bf16[1,256,5120]{2,1,0:T(8,128)(2,1)} %refs_1_.1), custom_call_target="tpu_custom_call" | custom-call | tf_op jit(solution)/shard_map/pallas_call | solution.py:743
  80.6 2.4 %shard_map.42 = (f32[2,1,40,128,128]{4,3,2,1,0:T(8,128)}, f32[1,2,40]{2,1,0:T(2,128)}) custom-call(f32[2,40,128,128]{3,2,1,0:T(8,128)S(1)} %get-tuple-element.4.w, f32[2,40]{1,0:T(2,128)S(1)} %get-tuple-element.5.sim), custom_call_target="tpu_custom_call" | custom-call | tf_op jit(solution)/shard_map/pallas_call | solution.py:782

commit v9 on v8

--- a/solution.py
+++ b/solution.py
@@ -635,7 +635,7 @@
         s3(name + "x", axis, (3,))
     for name in GATHERS:
         g4_arrive(name)
-    loop(HEADS, emit, unroll=2)
+    loop(HALF, emit, unroll=2)
     collected(0)
     for name in CHAINS:
         chain_left(name)
@@ -654,6 +654,7 @@
     for name in LATE:
         s3_sum(name + "x", False)
         s4(name + "x", False)
+    loop(HALF, lambda i: emit(HALF + i), unroll=2)
     pl.when(owner)(own_similarity)
 
     @pl.when(early_owner)
@@ -758,7 +759,7 @@
     )
 
 
-PIECES = 4
+PIECES = 1
 
 
 def store_kernel(w, sim, w_hbm, s_hbm, sems):

time: 83.1 us -> 82.3 us (level)
  no operation moved by 1% of the time
where the time goes in v9:
time: 82.3 us; the launch traced here: 82.2 us
  Pallas kernels  81.6 us (99%)
    pallas_call x1, Pallas kernels, gather_kernel(): pl.pallas_call(functools.partial(kernel, tokens, names), out_shape=(pltpu...  79.2 us
    pallas_call x1, Pallas kernels, store(): pl.pallas_call(store_kernel, out_shape=(jax.ShapeDtypeStruct((2, 1, HEADS...  2.39 us

profile of v9, /device:TPU:1, one launch (start us, length us, event | category | flops | bytes accessed | tf_op | source)
XLA Modules:
  0.0 82.2 jit_solution(17450916908900361905)
XLA Ops:
  0.6 79.2 %shard_map.41 = (f32[2,40,128,128]{3,2,1,0:T(8,128)S(1)}, f32[2,40]{1,0:T(2,128)S(1)}) custom-call(bf16[1,256,5120]{2,1,0:T(8,128)(2,1)} %refs_0_.1, bf16[1,256,5120]{2,1,0:T(8,128)(2,1)} %refs_1_.1), custom_call_target="tpu_custom_call" | custom-call | tf_op jit(solution)/shard_map/pallas_call | solution.py:744
  79.9 2.4 %shard_map.42 = (f32[2,1,40,128,128]{4,3,2,1,0:T(8,128)}, f32[1,2,40]{2,1,0:T(2,128)}) custom-call(f32[2,40,128,128]{3,2,1,0:T(8,128)S(1)} %get-tuple-element.4.w, f32[2,40]{1,0:T(2,128)S(1)} %get-tuple-element.5.sim), custom_call_target="tpu_custom_call" | custom-call | tf_op jit(solution)/shard_map/pallas_call | solution.py:783
